TPU v7x, 256 devices: a whole 4x4x8 slice. The times are simulated.
256 devices in a mesh: rows: 32 (over x, z), grp: 8 (over y, core).
Axes of the slice: x: 4, y: 4, z: 8, core: 2. Of those that a mesh axis runs over, the one named last changes fastest.
Arguments:
- sketch: float32 [2048, 65536], P(None, ('rows', 'grp')), may hold values from -0.125 to 0.125
- prior_basis: float32 [65536, 512], P(('rows', 'grp'))
- panel_block: float32 [65536, 256], P(('rows', 'grp'))
- panel_index: int32 [1], replicated, may hold values from 0 to 2
- prior_count: int32 [1], replicated, may hold values from 384 to 512
Outputs:
- new_basis: float32 [65536, 128], P(('rows', 'grp'))
- factors: float32 [640, 128], replicated
All inputs are finite; a program needn't handle non-finite values.
Results may differ from a plain program's by a relative error of at most 0.00011.
Values sent between devices are 32-bit elements; how exact they have to be, the bound alone decides.
A program may use at most 64 MiB of HBM per device.

v0:
```python
import functools

import jax
import jax.numpy as jnp
from jax import lax
from jax.sharding import Mesh
from jax.sharding import PartitionSpec as P

P_SIZE = 64
ROWS_GRP = ("rows_0", "rows_1", "grp_0", "grp_1")
ROWS = ("rows_0", "rows_1")
GRP = ("grp_0", "grp_1")


def by_axis(value, axes):
    return functools.reduce(lax.psum, axes, value)


def matmul(left, right):
    return jnp.dot(left, right, precision=lax.Precision.HIGHEST)


def right_solve(factor, values):
    return jax.scipy.linalg.solve_triangular(factor, values.T, lower=True).T


def shards(sketch, prior_basis, panel_block, panel_index, prior_count):
    width = prior_basis.shape[1]
    column_keep = (jnp.arange(width) < prior_count[0]).astype(jnp.float32)
    masked = prior_basis * column_keep
    start = panel_index[0] * P_SIZE
    chosen = lax.dynamic_slice_in_dim(panel_block, start, 2 * P_SIZE, 1)
    first = chosen[:, :P_SIZE]
    second = chosen[:, P_SIZE:]
    local_prior = matmul(sketch, masked)
    local_panels = matmul(sketch, chosen)
    prior_sketch = lax.psum(local_prior, ROWS_GRP)
    sketch_one = lax.psum(local_panels[:, :P_SIZE], ROWS_GRP)
    sketch_two = lax.psum(local_panels[:, P_SIZE:], ROWS_GRP)
    gram_prior = matmul(prior_sketch.T, prior_sketch) + jnp.diag(1.0 - column_keep)
    prior_factor = jnp.linalg.cholesky(gram_prior)
    coef_one = jax.scipy.linalg.cho_solve((prior_factor, True), matmul(prior_sketch.T, sketch_one))
    skres_one = sketch_one - matmul(prior_sketch, coef_one)
    coef_two = jax.scipy.linalg.cho_solve((prior_factor, True), matmul(prior_sketch.T, sketch_two))
    skres_two = sketch_two - matmul(prior_sketch, coef_two)
    resid_one = first - matmul(masked, coef_one)
    gram_first = by_axis(matmul(resid_one.T, resid_one), ROWS_GRP)
    tri_one = jnp.linalg.cholesky(gram_first)
    basis_one = right_solve(tri_one, resid_one)
    skbasis_one = right_solve(tri_one, skres_one)
    resid_two = second - matmul(masked, coef_two)
    small_gram = matmul(skbasis_one.T, skbasis_one)
    small_cross = matmul(skbasis_one.T, skres_two)
    small_factor = jnp.linalg.cholesky(small_gram)
    inner = jax.scipy.linalg.cho_solve((small_factor, True), small_cross)
    final_two = resid_two - matmul(basis_one, inner)
    gram_second = by_axis(matmul(final_two.T, final_two), ROWS_GRP)
    tri_two = jnp.linalg.cholesky(gram_second)
    basis_two = right_solve(tri_two, final_two)
    total_rows = prior_basis.shape[0] * lax.axis_size(ROWS) * lax.axis_size(GRP)
    scale_rows = jnp.sqrt(jnp.float32(total_rows))
    new_basis = jnp.concatenate([basis_one, basis_two], axis=1) * scale_rows
    upper = jnp.concatenate([tri_one.T, inner], axis=1)
    lower_rows = jnp.concatenate([jnp.zeros((P_SIZE, P_SIZE), jnp.float32), tri_two.T], axis=1)
    factors = jnp.concatenate(
        [jnp.concatenate([coef_one, coef_two], axis=1), upper, lower_rows], axis=0
    )
    return (new_basis, factors)


def solution(mesh):
    torus = Mesh(mesh.devices.reshape(4, 8, 4, 2), ("rows_0", "rows_1", "grp_0", "grp_1"))
    return jax.shard_map(
        shards,
        mesh=torus,
        in_specs=(P(None, ROWS_GRP), P(ROWS_GRP, None), P(ROWS_GRP, None), P(), P()),
        out_specs=(P(ROWS_GRP, None), P()),
        check_vma=False,
    )
```

profile of v0, /device:TPU:1, one launch (start us, length us, event | category | flops | bytes accessed | tf_op | source)
XLA Modules:
  0.0 663.9 jit_solution(3610918561015225058)
XLA Ops:
  8.8 3.3 convolution_bitcast_fusion.1
  12.1 1.1 fusion.115
  13.8 8.3 %convolution_bitcast_fusion = f32[2048,512]{0,1:T(8,128)} fusion(f32[2048,256]{1,0:T(8,128)S(1)} %copy-done, f32[256,512]{1,0:T(8,128)S(1)} %copy-done.6, f32[512]{0:T(512)S(1)} %fusion.100), kind=kOutput, calls=%fused_computation.2 | convolution fusion | flops 3221356544 | bytes 6817792 | tf_op jit(solution)/shard_map/dot_general | solution.py:20
  24.6 273.6 %all-reduce.5.cloned.1.call-done = (f32[2048,512]{0,1:T(8,128)}, f32[2048,64]{0,1:T(8,128)}, f32[2048,64]{0,1:T(8,128)}) async-done(((f32[2048,512]{0,1:T(8,128)}, f32[2048,64]{0,1:T(8,128)}, f32[2048,64]{0,1:T(8,128)}), (f32[2048,512]{0,1:T(8,128)}, f32[2048,64]{0,1:T(8,128)}, f32[2048,64]{0,1:T(8,128)})) %all-reduce.5.cloned.1.call-update) | async-done | bytes 5242896 | tf_op jit(solution)/shard_map/psum | solution.py:37
  298.2 9.5 %fusion.116 = f32[512,512]{1,0:T(8,128)S(1)} fusion(f32[2048,512]{0,1:T(8,128)} %get-tuple-element.31), kind=kOutput, calls=%fused_computation.194 | convolution fusion | flops 6442450944 | bytes 5242880 | tf_op jit(solution)/shard_map/dot_general | solution.py:20
  307.7 1.3 copy.8
  309.0 1.5 fusion.1
  311.5 11.7 %cholesky.119 = f32[128,128]{1,0:T(8,128)S(1)} custom-call(f32[128,128]{1,0:T(8,128)S(1)} %cholesky.353), custom_call_target="Cholesky" | custom-call | tf_op jit(solution)/shard_map/jit(cholesky)/cholesky | solution.py:41
  323.2 9.8 %custom-call.48 = f32[1,128,128]{1,2,0:T(8,128)S(1)} custom-call(f32[1,128,128]{2,1,0:T(8,128)S(1)} %get-tuple-element.49), custom_call_target="InvertDiagBlocksLowerTriangular" | custom-call | tf_op jit(solution)/shard_map/jit(cholesky)/cholesky | solution.py:41
  333.2 1.2 constant_dynamic-update-slice_fusion
  334.4 1.3 convolution_subtract_fusion.2
  335.7 11.7 %cholesky.242 = f32[128,128]{1,0:T(8,128)S(1)} custom-call(f32[128,128]{1,0:T(8,128)S(1)} %cholesky.357), custom_call_target="Cholesky" | custom-call | tf_op jit(solution)/shard_map/jit(cholesky)/cholesky | solution.py:41
  347.4 10.2 %custom-call.49 = f32[1,128,128]{1,2,0:T(8,128)S(1)} custom-call(f32[1,128,128]{2,1,0:T(8,128)S(1)} %get-tuple-element.46), custom_call_target="InvertDiagBlocksLowerTriangular" | custom-call | tf_op jit(solution)/shard_map/jit(cholesky)/cholesky | solution.py:41
  357.9 1.3 convolution_subtract_fusion.3
  359.2 11.7 %cholesky.263 = f32[128,128]{1,0:T(8,128)S(1)} custom-call(f32[128,128]{1,0:T(8,128)S(1)} %cholesky.362), custom_call_target="Cholesky" | custom-call | tf_op jit(solution)/shard_map/jit(cholesky)/cholesky | solution.py:41
  371.6 9.8 %custom-call.50 = f32[1,128,128]{1,2,0:T(8,128)S(1)} custom-call(f32[1,128,128]{2,1,0:T(8,128)S(1)} %get-tuple-element.43), custom_call_target="InvertDiagBlocksLowerTriangular" | custom-call | tf_op jit(solution)/shard_map/jit(cholesky)/cholesky | solution.py:41
  381.7 1.2 convolution_subtract_fusion.7
  382.9 11.7 %cholesky.280 = f32[128,128]{1,0:T(8,128)S(1)} custom-call(f32[128,128]{1,0:T(8,128)S(1)} %convolution_subtract_fusion.7), custom_call_target="Cholesky" | custom-call | tf_op jit(solution)/shard_map/jit(cholesky)/cholesky | solution.py:41
  398.8 1.5 select_select_fusion
  400.4 10.8 %while.4 = (s32[]{:T(128)}, f32[512,512]{1,0:T(8,128)S(1)}, s32[4,2]{0,1:T(2,128)S(1)}, f32[4,128,128]{2,1,0:T(8,128)}, s32[]{:T(128)}) while((s32[]{:T(128)}, f32[512,512]{1,0:T(8,128)S(1)}, s32[4,2]{0,1:T(2,128)S(1)}, f32[4,128,128]{2,1,0:T(8,128)}, s32[]{:T(128)}) %tuple.43), condition=%wide.while_cond, body=%wide.while_body.sunk | while | flops 2 | bytes 132705 | solution.py:42
  401.1 2.0 bitcast_dynamic-update-slice_fusion.2
  403.7 2.0 bitcast_dynamic-update-slice_fusion.2
  406.4 2.0 bitcast_dynamic-update-slice_fusion.2
  409.1 2.0 bitcast_dynamic-update-slice_fusion.2
  411.1 40.2 %custom-call.55 = f32[4,128,128]{1,2,0:T(8,128)S(1)} custom-call(f32[4,128,128]{2,1,0:T(8,128)} %get-tuple-element.19), custom_call_target="InvertDiagBlocksLowerTriangular" | custom-call | tf_op jit(solution)/shard_map/jit(_cho_solve)/triangular_solve | solution.py:42
  451.3 6.6 fusion.117
  461.5 3.7 convolution_subtract_fusion.1
  466.6 13.6 %psum.79 = f32[64,64]{0,1:T(8,128)S(1)} all-reduce(f32[64,64]{0,1:T(8,128)S(1)} %fusion.118), channel_id=1, replica_groups=mesh['rows_0'=4,'rows_1'=8,'grp_0'=4,'grp_1'=2] {'rows_0'}, use_global_device_ids=true, to_apply=%region_10.12 | all-reduce | flops 4096 | bytes 32768 | tf_op jit(solution)/shard_map/psum | solution.py:16
  480.2 23.5 %psum.80 = f32[64,64]{0,1:T(8,128)S(1)} all-reduce(f32[64,64]{0,1:T(8,128)S(1)} %psum.79), channel_id=1, replica_groups=mesh['rows_0'=4,'rows_1'=8,'grp_0'=4,'grp_1'=2] {'rows_1'}, use_global_device_ids=true, to_apply=%region_11.13 | all-reduce | flops 4096 | bytes 32768 | tf_op jit(solution)/shard_map/psum | solution.py:16
  503.7 12.5 %psum.81 = f32[64,64]{0,1:T(8,128)S(1)} all-reduce(f32[64,64]{0,1:T(8,128)S(1)} %psum.80), channel_id=1, replica_groups=mesh['rows_0'=4,'rows_1'=8,'grp_0'=4,'grp_1'=2] {'grp_0'}, use_global_device_ids=true, to_apply=%region_12.14 | all-reduce | flops 4096 | bytes 32768 | tf_op jit(solution)/shard_map/psum | solution.py:16
  516.3 16.3 %psum.82 = f32[64,64]{0,1:T(8,128)S(1)} all-reduce(f32[64,64]{0,1:T(8,128)S(1)} %psum.81), channel_id=1, replica_groups=mesh['rows_0'=4,'rows_1'=8,'grp_0'=4,'grp_1'=2] {'grp_1'}, use_global_device_ids=true, to_apply=%region_13.15 | all-reduce | flops 4096 | bytes 32768 | tf_op jit(solution)/shard_map/psum | solution.py:16
  532.7 5.8 cholesky.322
  539.2 1.2 fusion.98
  540.5 4.9 custom-call.56
  545.4 1.7 fusion.58
  547.1 1.7 fusion.93
  550.1 6.6 cholesky.333
  558.0 5.5 custom-call.52
  563.6 6.6 fusion.119
  570.3 1.1 convolution_subtract_fusion.13
  574.6 3.1 convolution_subtract_fusion
  579.4 1.1 convolution_subtract_fusion.4
  580.7 11.3 %psum.84 = f32[64,64]{0,1:T(8,128)S(1)} all-reduce(f32[64,64]{0,1:T(8,128)S(1)} %fusion.122), channel_id=1, replica_groups=mesh['rows_0'=4,'rows_1'=8,'grp_0'=4,'grp_1'=2] {'rows_0'}, use_global_device_ids=true, to_apply=%region_17.21 | all-reduce | flops 4096 | bytes 32768 | tf_op jit(solution)/shard_map/psum | solution.py:16
  592.0 20.7 %psum.85 = f32[64,64]{0,1:T(8,128)S(1)} all-reduce(f32[64,64]{0,1:T(8,128)S(1)} %psum.84), channel_id=1, replica_groups=mesh['rows_0'=4,'rows_1'=8,'grp_0'=4,'grp_1'=2] {'rows_1'}, use_global_device_ids=true, to_apply=%region_18.22 | all-reduce | flops 4096 | bytes 32768 | tf_op jit(solution)/shard_map/psum | solution.py:16
  612.7 11.6 %psum.86 = f32[64,64]{0,1:T(8,128)S(1)} all-reduce(f32[64,64]{0,1:T(8,128)S(1)} %psum.85), channel_id=1, replica_groups=mesh['rows_0'=4,'rows_1'=8,'grp_0'=4,'grp_1'=2] {'grp_0'}, use_global_device_ids=true, to_apply=%region_19.23 | all-reduce | flops 4096 | bytes 32768 | tf_op jit(solution)/shard_map/psum | solution.py:16
  624.3 17.2 %psum.87 = f32[64,64]{0,1:T(8,128)S(1)} all-reduce(f32[64,64]{0,1:T(8,128)S(1)} %psum.86), channel_id=1, replica_groups=mesh['rows_0'=4,'rows_1'=8,'grp_0'=4,'grp_1'=2] {'grp_1'}, use_global_device_ids=true, to_apply=%region_20.24 | all-reduce | flops 4096 | bytes 32768 | tf_op jit(solution)/shard_map/psum | solution.py:16
  641.6 5.8 cholesky.344
  650.6 4.9 custom-call.58
  (130 shorter events, 27.4 us)
Async XLA Ops:
  7.2 1.6 copy-start
  7.2 6.6 copy-start.6
  7.2 291.0 %all-reduce.5.cloned.1.call-start = ((), (), s32[]{:S(2)}) async-start(), calls=%async_computation | async-start | bytes 10485760 | tf_op jit(solution)/shard_map/psum | solution.py:37
  22.1 0.9 copy-start.15
  310.5 1.0 copy-start.9
  394.6 4.2 copy-start.5
  411.1 54.0 %copy-start.3 = (f32[512,512]{1,0:T(8,128)}, f32[512,512]{1,0:T(8,128)S(1)}, u32[]{:S(2)}) copy-start(f32[512,512]{1,0:T(8,128)S(1)} %get-tuple-element.112) | copy-start | bytes 3145732
  451.3 10.1 %copy-start.1 = (f32[2048,512]{0,1:T(8,128)S(1)}, f32[2048,512]{0,1:T(8,128)}, u32[]{:S(2)}) copy-start(f32[2048,512]{0,1:T(8,128)} %get-tuple-element.31) | copy-start | bytes 12582916
  451.3 10.1 %copy-start.11 = (f32[2048,64]{0,1:T(8,128)S(1)}, f32[2048,64]{0,1:T(8,128)}, u32[]{:S(2)}) copy-start(f32[2048,64]{0,1:T(8,128)} %get-tuple-element.33) | copy-start | bytes 1572868
  457.9 7.2 %copy-start.7 = (f32[256,512]{1,0:T(8,128)S(1)}, f32[256,512]{1,0:T(8,128)}, u32[]{:S(2)}) copy-start(f32[256,512]{1,0:T(8,128)} %param.11) | copy-start | bytes 1572868
  457.9 7.2 %copy-start.20 = (f32[256,64]{0,1:T(8,128)S(1)}, f32[256,64]{0,1:T(8,128)}, u32[]{:S(2)}) copy-start(f32[256,64]{0,1:T(8,128)} %copy.20) | copy-start | bytes 196612
  460.9 87.9 %copy-start.13 = (f32[128,64]{0,1:T(8,128)}, f32[128,64]{0,1:T(8,128)S(1)}, u32[]{:S(2)}) copy-start(f32[128,64]{0,1:T(8,128)S(1)} %fusion.73) | copy-start | bytes 98308
  461.5 4.3 copy-start.17
  465.8 0.6 copy-start.12
  548.8 25.7 %copy-start.10 = (f32[2048,64]{0,1:T(8,128)S(1)}, f32[2048,64]{0,1:T(8,128)}, u32[]{:S(2)}) copy-start(f32[2048,64]{0,1:T(8,128)} %get-tuple-element.32) | copy-start | bytes 1572868
  563.5 8.1 %copy-start.4 = (f32[512,512]{1,0:T(8,128)S(1)}, f32[512,512]{1,0:T(8,128)}, u32[]{:S(2)}) copy-start(f32[512,512]{1,0:T(8,128)} %copy-done.3) | copy-start | bytes 3145732
  563.6 11.0 %copy-start.2 = (f32[2048,512]{0,1:T(8,128)S(1)}, f32[2048,512]{0,1:T(8,128)}, u32[]{:S(2)}) copy-start(f32[2048,512]{0,1:T(8,128)} %get-tuple-element.31) | copy-start | bytes 12582916
  571.9 6.3 copy-start.21
  572.1 6.6 copy-start.8
  572.1 6.6 copy-start.19
  574.0 4.7 copy-start.14
  574.6 4.1 copy-start.18
  577.6 78.1 %copy-start.16 = (f32[64,256]{1,0:T(8,128)S(1)}, f32[64,256]{1,0:T(8,128)}, u32[]{:S(2)}) copy-start(f32[64,256]{1,0:T(8,128)} %fusion.58) | copy-start | bytes 196612
Sparse Core Ops, SparseCore 0:
  22.2 275.9 all-reduce.4
where the time goes:
time: 672 us; the launch traced here: 664 us
  waiting for transfers between devices  274 us (41%)
  other arithmetic  162 us (24%)
  blocking collectives  127 us (19%)
  matrix products  62 us (9%)
  local copies, waits for them, and re-layouts  20.1 us (3%)
  between operations  19.3 us (3%)
    psum x1, waiting for transfers between devices, shards(): prior_sketch = lax.psum(local_prior, ROWS_GRP)  274 us
    psum x8, blocking collectives, by_axis(): return functools.reduce(lax.psum, axes, value)  127 us
    another operation x14, other arithmetic, shards(): prior_factor = jnp.linalg.cholesky(gram_prior)  79 us
    dot_general x14, matrix products, matmul(): return jnp.dot(left, right, precision=lax.Precision.HIGHEST)  44.9 us
    another operation x4, other arithmetic, shards(): jax.scipy.linalg.cho_solve((prior_factor, True), matmul(prior_sketch.T, s...  41.7 us
  transfers between devices with their start and end apart: 1, of which 1 were waited for; matrix products, arithmetic and copies ran while one was open for 0% of the time, Pallas kernels for 0%

commit v1 on v0

v1 whole, which is shorter than its diff:
```python
import jax
import jax.numpy as jnp
from jax import lax
from jax.experimental import pallas as pl
from jax.experimental.pallas import tpu as pltpu
from jax.sharding import Mesh
from jax.sharding import PartitionSpec as P

P_SIZE = 64
AXES = ("x", "z", "y", "c")
MESH = pl.DeviceIdType.MESH
F32 = jnp.float32
BF16 = jnp.bfloat16


def vmem():
    return pl.BlockSpec(memory_space=pltpu.VMEM)


def dot(left, right):
    return jnp.dot(left, right, precision=lax.Precision.HIGHEST, preferred_element_type=F32)


def dot_rows(left, right):
    return lax.dot_general(
        left, right, (((0,), (0,)), ((), ())), precision=lax.Precision.HIGHEST, preferred_element_type=F32
    )


def split(value):
    high = value.astype(BF16)
    return high, (value - high.astype(F32)).astype(BF16)


def halves(place):
    first = (place + 1) - 2 * lax.rem(place, 2)
    second = lax.rem(place + 3 + 2 * lax.rem(place, 2), 4)
    return (first, lax.rem((place + 1) // 2, 2)), (second, place // 2)


def gram_kernel(sketch, wide, out, high, low, away, came, acc, r0, r1, r2, r3, zout, zin, zall, full, mine, other,
                d_send, d_recv, r_send, r_recv, z_send, z_recv, y_send, y_recv, a_send, a_recv, m_send, m_recv):
    x, z, y, c = (lax.axis_index(name) for name in AXES)
    (xa, xa_bit), (xb, xb_bit) = halves(x)
    (ya, ya_bit), (yb, yb_bit) = halves(y)
    links = (({"x": xa}, xa_bit), ({"y": ya}, ya_bit), ({"x": xb}, xb_bit), ({"y": yb}, yb_bit))
    ring = [{"z": lax.rem(z + step, 8)} for step in range(1, 8)]
    peer = {"c": 1 - c}

    barrier = pltpu.get_barrier_semaphore()
    for target in [peer] + [link for link, _ in links] + ring:
        pl.semaphore_signal(barrier, inc=1, device_id=target, device_id_type=MESH)

    def remote(source, target, send, recv, device):
        return pltpu.make_async_remote_copy(
            src_ref=source, dst_ref=target, send_sem=send, recv_sem=recv, device_id=device, device_id_type=MESH
        )

    starts, sent = [], []
    for s in range(4):
        at, kept, gone = 0, [0], []
        for t in range(4):
            size = 16 >> t
            bit = links[(s + t) % 4][1]
            gone.append(at + (1 - bit) * size)
            at = at + bit * size
            kept.append(at)
        starts.append(kept)
        sent.append(gone)

    wide_high, wide_low = split(wide[...])
    high[...] = wide_high
    low[...] = wide_low

    def product(row):
        part_high, part_low = split(sketch[pl.ds(pl.multiple_of(row, 128), 128), :])
        value = jnp.dot(part_high, low[...], preferred_element_type=F32)
        value = value + jnp.dot(part_low, high[...], preferred_element_type=F32)
        return value + jnp.dot(part_high, high[...], preferred_element_type=F32)

    def spot(i):
        s, kept = lax.rem(i, 4), i // 4
        bit = lax.rem(s, 2) * (ya_bit * (1 - s // 2) + yb_bit * (s // 2))
        bit = bit + (1 - lax.rem(s, 2)) * (xa_bit * (1 - s // 2) + xb_bit * (s // 2))
        return s, 16 * (kept * bit + (1 - kept) * (1 - bit))

    def chunk(i):
        s, tile = spot(i)
        return remote(away.at[s, pl.ds(tile, 16)], came.at[s, pl.ds(tile, 16)], d_send.at[i], d_recv.at[i], peer)

    def for_peer(i, carry):
        s, tile = spot(i)
        away[s, pl.ds(tile, 16)] = product((1 - c) * 1024 + s * 256 + tile * 8).reshape(16, 8, 640)

        @pl.when(i == 0)
        def _():
            pl.semaphore_wait(barrier, 12)

        chunk(i).start()
        return carry

    def for_self(i, carry):
        s, tile = spot(i)
        acc[s, pl.ds(tile, 16)] = product(c * 1024 + s * 256 + tile * 8).reshape(16, 8, 640)
        return carry

    lax.fori_loop(0, 8, for_peer, 0)
    lax.fori_loop(0, 8, for_self, 0)

    landing = (r0, r1, r2, r3)

    def scatter(t, s):
        size = 16 >> t
        return remote(
            acc.at[s, pl.ds(sent[s][t], size)], landing[t].at[s], r_send.at[t, s], r_recv.at[t, s],
            links[(s + t) % 4][0],
        )

    for i in range(8):
        s, tile = spot(i)
        chunk(i).wait_recv()
        acc[s, pl.ds(tile, 16)] += came[s, pl.ds(tile, 16)]
        if i < 4:
            scatter(0, i).start()
    for t in range(4):
        size = 16 >> t
        for s in range(4):
            scatter(t, s).wait_recv()
            at = starts[s][t + 1]
            if t < 3:
                acc[s, pl.ds(at, size)] += landing[t][s]
                scatter(t + 1, s).start()
            else:
                zout[pl.ds(2 * s, 2)] = acc[s, pl.ds(at, 2)] + r3[s]

    def along(step):
        return remote(
            zout.at[lax.rem(z + step, 8)], zin.at[step - 1], z_send.at[step - 1], z_recv.at[step - 1], ring[step - 1]
        )

    def back(step):
        return remote(zall.at[z], zall.at[z], y_send.at[step - 1], y_recv.at[step - 1], ring[step - 1])

    for step in range(1, 8):
        along(step).start()
    total = zout[z]
    for step in range(1, 8):
        along(step).wait_recv()
        total = total + zin[step - 1]
    zall[z] = total
    for step in range(1, 8):
        back(step).start()
    for step in range(1, 8):
        back(step).wait_recv()

    def gather(t, s):
        size = 16 >> t
        here = full.at[s, pl.ds(starts[s][t + 1], size)]
        source = zall.at[pl.ds(2 * s, 2)] if t == 3 else here
        return remote(source, here, a_send.at[t, s], a_recv.at[t, s], links[(s + t) % 4][0])

    for s in range(4):
        gather(3, s).start()
    for s in range(4):
        full[s, pl.ds(starts[s][4], 2)] = zall[pl.ds(2 * s, 2)]
    for t in (2, 1, 0):
        for s in range(4):
            gather(t + 1, s).wait_recv()
            gather(t, s).start()

    def add_gram(rows, first):
        part_high, part_low = split(rows)
        for i in range(5):
            lo = 128 * i
            value = None
            for left in (part_low, part_high):
                for right in (part_low, part_high):
                    term = lax.dot_general(
                        left[:, lo:lo + 128], right[:, lo:], (((0,), (0,)), ((), ())), preferred_element_type=F32
                    )
                    value = term if value is None else value + term
            if first:
                mine[lo:lo + 128, lo:] = value
            else:
                mine[lo:lo + 128, lo:] += value

    add_gram(jnp.concatenate([full[s, pl.ds(starts[s][1], 16)].reshape(128, 640) for s in range(4)], axis=0), True)
    for s in (0, 2):
        rows = []
        for u in (s, s + 1):
            gather(0, u).wait_recv()
            rows.append(full[u, pl.ds(sent[u][0], 16)].reshape(128, 640))
        add_gram(jnp.concatenate(rows, axis=0), False)

    def swap(i):
        lo = 128 * i
        return remote(
            mine.at[pl.ds(lo, 128), pl.ds(lo, 640 - lo)], other.at[pl.ds(lo, 128), pl.ds(lo, 640 - lo)],
            m_send.at[i], m_recv.at[i], peer,
        )

    for i in range(5):
        swap(i).start()
    for i in range(5):
        lo = 128 * i
        swap(i).wait_recv()
        out[lo:lo + 128, lo:] = mine[lo:lo + 128, lo:] + other[lo:lo + 128, lo:]
        if i:
            out[lo:lo + 128, :lo] = jnp.zeros((128, lo), F32)

    for i in range(8):
        chunk(i).wait_send()
    for t in range(4):
        for s in range(4):
            scatter(t, s).wait_send()
            gather(t, s).wait_send()
    for step in range(1, 8):
        along(step).wait_send()
        back(step).wait_send()
    for i in range(5):
        swap(i).wait_send()


def sketch_gram(sketch, wide):
    dma = pltpu.SemaphoreType.DMA
    scratch = [pltpu.VMEM((256, 640), BF16)] * 2
    scratch += [pltpu.VMEM((4, 32, 8, 640), F32)] * 3
    scratch += [pltpu.VMEM((4, 16 >> t, 8, 640), F32) for t in range(4)]
    scratch += [pltpu.VMEM((8, 8, 640), F32), pltpu.VMEM((7, 8, 640), F32), pltpu.VMEM((8, 8, 640), F32)]
    scratch += [pltpu.VMEM((4, 32, 8, 640), F32)]
    scratch += [pltpu.VMEM((640, 640), F32)] * 2
    scratch += [dma((8,))] * 2 + [dma((4, 4))] * 2 + [dma((7,))] * 4 + [dma((4, 4))] * 2 + [dma((5,))] * 2
    return pl.pallas_call(
        gram_kernel,
        out_shape=jax.ShapeDtypeStruct((640, 640), F32),
        in_specs=[vmem()] * 2,
        out_specs=vmem(),
        scratch_shapes=scratch,
        compiler_params=pltpu.CompilerParams(
            collective_id=0, has_side_effects=True, vmem_limit_bytes=48 * 1024 * 1024
        ),
        name="sketch_gram",
    )(sketch, wide)


def sweep(blocks, panels):
    blocks = list(blocks)
    lane = lax.broadcasted_iota(jnp.int32, (8, 128), 1)
    row = lax.broadcasted_iota(jnp.int32, (8, 128), 0)
    for p in range(panels):
        k = 8 * p
        inside = (lane >= k) & (lane < k + 8)
        cols = [[jnp.broadcast_to(b[:, k + s:k + s + 1], (8, 128)) for s in range(8)] for b in blocks]
        e = list(cols[p])
        r = jnp.where(inside, (lane - k == row).astype(F32), blocks[p])
        for s in range(8):
            inv = 1.0 / e[s][s:s + 1, :]
            rs = r[s:s + 1, :] * inv
            r = jnp.where(row == s, rs, r - e[s] * rs)
            for u in range(s + 1, 8):
                es = e[u][s:s + 1, :] * inv
                e[u] = jnp.where(row == s, es, e[u] - e[s] * es)
        rows = [r[s:s + 1, :] for s in range(8)]
        for i in range(len(blocks)):
            if i == p:
                continue
            total = jnp.where(inside, 0.0, blocks[i])
            for s in range(8):
                total = total - cols[i][s] * rows[s]
            blocks[i] = total
        blocks[p] = r
    return blocks


def solve_kernel(count, gram, wide, coef, resid, small, a):
    r = lax.broadcasted_iota(jnp.int32, (128, 128), 0)
    c = lax.broadcasted_iota(jnp.int32, (128, 128), 1)
    a[...] = gram[...]
    for k in range(4):
        lo = 128 * k
        hi = lo + 128
        unused = (c + lo >= count[0]) & (r == c)
        block = a[lo:hi, lo:hi] + jnp.where(unused, 1.0, 0.0)
        inverse = jnp.concatenate(sweep([block[8 * i:8 * i + 8] for i in range(16)], 16), axis=0)
        y = dot(inverse, a[lo:hi, hi:])
        for i in range(k + 1, 5):
            left = 128 * i
            a[left:left + 128, left:] -= dot_rows(a[lo:hi, left:left + 128], y[:, left - hi:])
        if k:
            a[:lo, hi:] -= dot(a[:lo, lo:hi], y)
        a[lo:hi, hi:] = y
    coefs = a[:512, 512:]
    tail = a[512:, 512:]
    both = jnp.concatenate(sweep([tail[8 * i:8 * i + 8] for i in range(8)], 8), axis=0)
    ratio = both[:, P_SIZE:]
    coef[0:512, :] = coefs
    coef[512:576, :] = both
    left = wide[:, 512:] - dot(wide[:, :512], coefs)
    first = left[:, :P_SIZE]
    second = left[:, P_SIZE:] - dot(first, ratio)
    final = jnp.concatenate([first, second], axis=1)
    resid[...] = final
    own = dot_rows(final, final)
    small[...] = jnp.concatenate([own[:P_SIZE, :P_SIZE], own[P_SIZE:, P_SIZE:]], axis=1)


def solve(count, gram, wide):
    return pl.pallas_call(
        solve_kernel,
        out_shape=(
            jax.ShapeDtypeStruct((576, 128), F32),
            jax.ShapeDtypeStruct((256, 128), F32),
            jax.ShapeDtypeStruct((64, 128), F32),
        ),
        in_specs=[pl.BlockSpec(memory_space=pltpu.SMEM), vmem(), vmem()],
        out_specs=(vmem(),) * 3,
        scratch_shapes=[pltpu.VMEM((640, 640), F32)],
        compiler_params=pltpu.CompilerParams(vmem_limit_bytes=32 * 1024 * 1024),
        name="solve",
    )(count, gram, wide)


def sum_kernel(small, out, peer_in, half, x_in, xy, y_in, xyz, z_in, done,
               p_send, p_recv, x_send, x_recv, y_send, y_recv, z_send, z_recv, b_send, b_recv):
    x, z, y, c = (lax.axis_index(name) for name in AXES)
    peer = {"c": 1 - c}
    xs = [{"x": lax.rem(x + step, 4)} for step in range(1, 4)]
    ys = [{"y": lax.rem(y + step, 4)} for step in range(1, 4)]
    zs = [{"z": lax.rem(z + step, 8)} for step in range(1, 8)]
    barrier = pltpu.get_barrier_semaphore()
    for target in [peer] + xs + ys + zs:
        pl.semaphore_signal(barrier, inc=1, device_id=target, device_id_type=MESH)
    pl.semaphore_wait(barrier, 14)

    def remote(source, target, send, recv, device):
        return pltpu.make_async_remote_copy(
            src_ref=source, dst_ref=target, send_sem=send, recv_sem=recv, device_id=device, device_id_type=MESH
        )

    def exchange(source, target, send, recv, devices):
        return [remote(source, target.at[i], send.at[i], recv.at[i], device) for i, device in enumerate(devices)]

    theirs = pl.ds(pl.multiple_of(32 * (1 - c), 32), 32)
    ours = pl.ds(pl.multiple_of(32 * c, 32), 32)
    across = remote(small.at[theirs], peer_in, p_send, p_recv, peer)
    across.start()
    across.wait_recv()
    half[...] = small[ours, :] + peer_in[...]
    on_x = exchange(half, x_in, x_send, x_recv, xs)
    for copy in on_x:
        copy.start()
    for copy in on_x:
        copy.wait_recv()
    xy[...] = half[...] + x_in[0] + x_in[1] + x_in[2]
    on_y = exchange(xy, y_in, y_send, y_recv, ys)
    for copy in on_y:
        copy.start()
    for copy in on_y:
        copy.wait_recv()
    xyz[...] = xy[...] + y_in[0] + y_in[1] + y_in[2]
    on_z = exchange(xyz, z_in, z_send, z_recv, zs)
    for copy in on_z:
        copy.start()
    total = xyz[...]
    for copy in on_z:
        copy.wait_recv()
    for i in range(7):
        total = total + z_in[i]
    done[...] = total
    out[ours, :] = total
    back = remote(done, out.at[ours], b_send, b_recv, peer)
    back.start()
    back.wait_recv()
    for copy in [across, back] + on_x + on_y + on_z:
        copy.wait_send()


def sum_small(small):
    dma = pltpu.SemaphoreType.DMA
    block = (32, 128)
    return pl.pallas_call(
        sum_kernel,
        out_shape=jax.ShapeDtypeStruct((64, 128), F32),
        in_specs=[vmem()],
        out_specs=vmem(),
        scratch_shapes=[
            pltpu.VMEM(block, F32), pltpu.VMEM(block, F32), pltpu.VMEM((3,) + block, F32), pltpu.VMEM(block, F32),
            pltpu.VMEM((3,) + block, F32), pltpu.VMEM(block, F32), pltpu.VMEM((7,) + block, F32), pltpu.VMEM(block, F32),
            dma, dma, dma((3,)), dma((3,)), dma((3,)), dma((3,)), dma((7,)), dma((7,)), dma, dma,
        ],
        compiler_params=pltpu.CompilerParams(collective_id=1, has_side_effects=True),
        name="sum_small",
    )(small)


def shards(sketch, prior_basis, panel_block, panel_index, prior_count):
    width = prior_basis.shape[1]
    column_keep = (jnp.arange(width) < prior_count[0]).astype(F32)
    chosen = lax.dynamic_slice_in_dim(panel_block, panel_index[0] * P_SIZE, 2 * P_SIZE, 1)
    wide = jnp.concatenate([prior_basis * column_keep, chosen], axis=1)
    gram = sketch_gram(sketch, wide)
    coef, resid, small = solve(prior_count, gram, wide)
    grams = sum_small(small)
    total_rows = prior_basis.shape[0] * 256
    scale_rows = jnp.sqrt(jnp.float32(total_rows))
    tri_one = jnp.linalg.cholesky(grams[:, :P_SIZE])
    tri_two = jnp.linalg.cholesky(grams[:, P_SIZE:])
    basis_one = jax.scipy.linalg.solve_triangular(tri_one, resid[:, :P_SIZE].T, lower=True).T
    basis_two = jax.scipy.linalg.solve_triangular(tri_two, resid[:, P_SIZE:].T, lower=True).T
    inner = jnp.dot(tri_one.T, coef[512:, P_SIZE:], precision=lax.Precision.HIGHEST)
    new_basis = jnp.concatenate([basis_one, basis_two], axis=1) * scale_rows
    upper = jnp.concatenate([tri_one.T, inner], axis=1)
    lower = jnp.concatenate([jnp.zeros((P_SIZE, P_SIZE), F32), tri_two.T], axis=1)
    return new_basis, jnp.concatenate([coef[:512], upper, lower], axis=0)


def solution(mesh):
    torus = Mesh(mesh.devices.reshape(4, 8, 4, 2), AXES)
    return jax.shard_map(
        shards,
        mesh=torus,
        in_specs=(P(None, AXES), P(AXES, None), P(AXES, None), P(), P()),
        out_specs=(P(AXES, None), P()),
        check_vma=False,
    )
```

time: 672 us -> 152 us (0.23); the launches traced: 664 us -> 152 us
  waiting for transfers between devices: 274 us -> 0 us
  other arithmetic: 162 us -> 27.2 us
  blocking collectives: 127 us -> 0 us
  Pallas kernels: 0 us -> 118 us
  matrix products: 62 us -> 1.63 us
  local copies, waits for them, and re-layouts: 20.1 us -> 2.7 us
  between operations: 19.3 us -> 2.23 us
    psum x1 -> x0, waiting for transfers between devices: 274 us -> none  [shards(): prior_sketch = lax.psum(local_prior, ROWS_GRP)]
    another operation x31 -> x8, other arithmetic: 157 us -> 23 us  [the longest x3 6.68 us: shards(): tri_one = jnp.linalg.cholesky(grams[:, :P_SIZE])]
    psum x8 -> x0, blocking collectives: 127 us -> none  [by_axis(): return functools.reduce(lax.psum, axes, value)]
    pallas_call x0 -> x3, Pallas kernels: none -> 118 us  [the longest x1 75.2 us: sketch_gram(): pl.pallas_call(gram_kernel, out_shape=jax.ShapeDtypeStruct((640, 640), F3...]
    dot_general x14 -> x1, matrix products: 44.9 us -> 0.95 us  [shards(): jnp.dot(tri_one.T, coef[512:, P_SIZE:], precision=lax.Precision.HIGHEST)]
    another operation x39 -> x2, matrix products: 17.2 us -> 0.67 us  [the longest x1 0.36 us: shards(): jax.scipy.linalg.solve_triangular(tri_two, resid[:, P_SIZE:].T, lower=True)]
    another operation x18 -> x0, local copies, waits for them, and re-layouts: 11 us -> none  [the longest x13 10.7 us: shards(): jax.scipy.linalg.cho_solve((prior_factor, True), matmul(prior_sketch.T, s...]
  transfers between devices with their start and end apart: 1 -> 0, of which waited for: 1 -> 0; matrix products, arithmetic and copies ran while one was open for 0% -> 0% of each run, Pallas kernels for 0% -> 0%
where the time goes in v1:
time: 152 us
  Pallas kernels  118 us (78%)
  other arithmetic  27.2 us (18%)
  local copies, waits for them, and re-layouts  2.7 us (2%)
  between operations  2.23 us (1%)
  matrix products  1.63 us (1%)
    pallas_call x1, Pallas kernels, sketch_gram(): pl.pallas_call(gram_kernel, out_shape=jax.ShapeDtypeStruct((640, 640), F3...  75.2 us
    pallas_call x1, Pallas kernels, solve(): pl.pallas_call(solve_kernel, out_shape=(jax.ShapeDtypeStruct((576, 128),...  22.6 us
    pallas_call x1, Pallas kernels, sum_small(): pl.pallas_call(sum_kernel, out_shape=jax.ShapeDtypeStruct((64, 128), F32)...  20 us
    another operation x3, other arithmetic, shards(): tri_one = jnp.linalg.cholesky(grams[:, :P_SIZE])  6.68 us
    another operation x3, other arithmetic, shards(): tri_two = jnp.linalg.cholesky(grams[:, P_SIZE:])  6.52 us
    another operation x1, other arithmetic, shards(): jax.scipy.linalg.solve_triangular(tri_two, resid[:, P_SIZE:].T, lower=True)  4.91 us
    another operation x1, other arithmetic, shards(): jax.scipy.linalg.solve_triangular(tri_one, resid[:, :P_SIZE].T, lower=True)  4.89 us

profile of v1, /device:TPU:1, one launch (start us, length us, event | category | flops | bytes accessed | tf_op | source)
XLA Modules:
  0.0 151.7 jit_solution(17315395599663153800)
XLA Ops:
  0.6 0.0 copy-start
  0.6 0.0 copy-start.1
  2.1 0.0 copy-done
  2.1 0.1 constant_dynamic-slice_fusion
  2.2 1.1 broadcast_multiply_fusion
  3.4 0.0 copy-done.1
  3.4 75.2 %sketch_gram.1.gram = f32[640,640]{1,0:T(8,128)S(1)} custom-call(f32[2048,256]{1,0:T(8,128)S(1)} %copy-done.1, f32[256,640]{1,0:T(8,128)S(1)} %pad_maximum_fusion.wide), custom_call_target="tpu_custom_call" | custom-call | tf_op jit(solution)/shard_map/sketch_gram/pallas_call | solution.py:233
  78.6 22.6 %solve.1 = (f32[576,128]{1,0:T(8,128)S(1)}, f32[256,128]{1,0:T(8,128)S(1)}, f32[64,128]{1,0:T(8,128)S(1)}) custom-call(s32[1]{0:T(128)} %copy.20.count, f32[640,640]{1,0:T(8,128)S(1)} %sketch_gram.1.gram, f32[256,640]{1,0:T(8,128)S(1)} %pad_maximum_fusion.wide), custom_call_target="tpu_custom_call" | custom-call | tf_op jit(solution)/shard_map/solve/pallas_call | solution.py:308
  101.3 0.0 copy-start.2
  101.3 0.6 copy-done.2
  101.9 20.0 %sum_small.1 = f32[64,128]{1,0:T(8,128)} custom-call(f32[64,128]{1,0:T(8,128)} %copy-done.2), custom_call_target="tpu_custom_call" | custom-call | tf_op jit(solution)/shard_map/sum_small/pallas_call | solution.py:381
  121.9 0.9 fusion.20
  122.8 0.1 copy.16
  122.9 0.1 copy.17
  123.0 0.9 fusion.7
  123.9 6.0 %cholesky.44 = f32[64,64]{1,0:T(8,128)S(1)} custom-call(f32[64,64]{1,0:T(8,128)S(1)} %get-tuple-element.16), custom_call_target="Cholesky" | custom-call | tf_op jit(solution)/shard_map/jit(cholesky)/cholesky | solution.py:406
  130.0 0.6 compare_reduce_fusion.1
  130.6 5.8 %cholesky.55 = f32[64,64]{1,0:T(8,128)S(1)} custom-call(f32[64,64]{1,0:T(8,128)S(1)} %get-tuple-element.17), custom_call_target="Cholesky" | custom-call | tf_op jit(solution)/shard_map/jit(cholesky)/cholesky | solution.py:407
  136.5 0.6 compare_reduce_fusion
  137.1 0.7 fusion.11
  137.8 0.1 copy.18
  137.9 4.9 %custom-call.7 = f32[1,64,64]{1,2,0:T(8,128)S(1)} custom-call(f32[1,64,64]{2,1,0:T(8,128)S(1)} %get-tuple-element.15), custom_call_target="InvertDiagBlocksLowerTriangular" | custom-call | tf_op jit(solution)/shard_map/jit(_solve_triangular)/triangular_solve | solution.py:409
  142.8 0.4 convolution_bitcast_fusion
  143.1 1.0 fusion.9
  144.1 0.7 fusion.13
  144.8 0.1 copy.12
  144.9 0.8 select_maximum_fusion
  145.7 4.9 %custom-call.6 = f32[1,64,64]{1,2,0:T(8,128)S(1)} custom-call(f32[1,64,64]{2,1,0:T(8,128)S(1)} %get-tuple-element.13), custom_call_target="InvertDiagBlocksLowerTriangular" | custom-call | tf_op jit(solution)/shard_map/jit(_solve_triangular)/triangular_solve | solution.py:408
  150.6 0.3 convolution_bitcast_fusion.1
  150.9 0.8 copy.14
  (7 shorter events, 0.2 us)
Async XLA Ops:
  0.6 1.5 copy-start
  0.6 2.8 %copy-start.1 = (f32[2048,256]{1,0:T(8,128)S(1)}, f32[2048,256]{1,0:T(8,128)}, u32[]{:S(2)}) copy-start(f32[2048,256]{1,0:T(8,128)} %sketch.1) | copy-start | bytes 6291460
  101.3 0.6 copy-start.2

commit v2 on v1

--- a/solution.py
+++ b/solution.py
@@ -1,3 +1,6 @@
+import functools
+import math
+
 import jax
 import jax.numpy as jnp
 from jax import lax
@@ -393,6 +396,66 @@
     )(small)
 
 
+def finish_kernel(scale, small, coef, resid, basis, factors):
+    lane = lax.broadcasted_iota(jnp.int32, (8, 128), 1)
+    row = lax.broadcasted_iota(jnp.int32, (8, 128), 0)
+    left = lane < P_SIZE
+    place = jnp.where(left, lane, lane - P_SIZE)
+    blocks = [small[8 * i:8 * i + 8, :] for i in range(8)]
+    extra = [(place == row + 8 * i).astype(F32) for i in range(8)]
+    roots, inverses = [], []
+    for p in range(8):
+        k = 8 * p
+
+        def column(block, s):
+            first = jnp.broadcast_to(block[:, k + s:k + s + 1], (8, 128))
+            second = jnp.broadcast_to(block[:, P_SIZE + k + s:P_SIZE + k + s + 1], (8, 128))
+            return jnp.where(left, first, second)
+
+        cols = {i: [column(blocks[i], s) for s in range(8)] for i in range(p, 8)}
+        e = list(cols[p])
+        r, q = blocks[p], extra[p]
+        for s in range(8):
+            pivot = e[s][s:s + 1, :]
+            inv = 1.0 / pivot
+            root = lax.rsqrt(pivot)
+            roots.append(jnp.where(place[:1] >= k + s, r[s:s + 1, :] * root, 0.0))
+            inverses.append(q[s:s + 1, :] * root)
+            rs, qs = r[s:s + 1, :] * inv, q[s:s + 1, :] * inv
+            here = row == s
+            r = jnp.where(here, rs, r - e[s] * rs)
+            q = jnp.where(here, qs, q - e[s] * qs)
+            for u in range(s + 1, 8):
+                es = e[u][s:s + 1, :] * inv
+                e[u] = jnp.where(here, es, e[u] - e[s] * es)
+        for i in range(p + 1, 8):
+            for s in range(8):
+                blocks[i] = blocks[i] - cols[i][s] * r[s:s + 1, :]
+                extra[i] = extra[i] - cols[i][s] * q[s:s + 1, :]
+    tri = jnp.concatenate(roots, axis=0)
+    inverse = jnp.concatenate(inverses, axis=0)
+    on_left = lax.broadcasted_iota(jnp.int32, (64, 128), 1) < P_SIZE
+    both = jnp.concatenate([jnp.where(on_left, inverse, 0.0), jnp.where(on_left, 0.0, inverse)], axis=0)
+    basis[...] = scale * lax.dot_general(
+        resid[...], both, (((1,), (1,)), ((), ())), precision=lax.Precision.HIGHEST, preferred_element_type=F32
+    )
+    tri_one = jnp.where(on_left, tri, 0.0)
+    ratio = jnp.where(on_left, 0.0, coef[512:576, :])
+    factors[0:512, :] = coef[0:512, :]
+    factors[512:576, :] = tri_one + dot(tri_one[:, :P_SIZE], ratio)
+    factors[576:640, :] = jnp.where(on_left, 0.0, tri)
+
+
+def finish(scale, small, coef, resid):
+    return pl.pallas_call(
+        functools.partial(finish_kernel, scale),
+        out_shape=(jax.ShapeDtypeStruct((256, 128), F32), jax.ShapeDtypeStruct((640, 128), F32)),
+        in_specs=[vmem()] * 3,
+        out_specs=(vmem(),) * 2,
+        name="finish",
+    )(small, coef, resid)
+
+
 def shards(sketch, prior_basis, panel_block, panel_index, prior_count):
     width = prior_basis.shape[1]
     column_keep = (jnp.arange(width) < prior_count[0]).astype(F32)
@@ -400,18 +463,8 @@
     wide = jnp.concatenate([prior_basis * column_keep, chosen], axis=1)
     gram = sketch_gram(sketch, wide)
     coef, resid, small = solve(prior_count, gram, wide)
-    grams = sum_small(small)
-    total_rows = prior_basis.shape[0] * 256
-    scale_rows = jnp.sqrt(jnp.float32(total_rows))
-    tri_one = jnp.linalg.cholesky(grams[:, :P_SIZE])
-    tri_two = jnp.linalg.cholesky(grams[:, P_SIZE:])
-    basis_one = jax.scipy.linalg.solve_triangular(tri_one, resid[:, :P_SIZE].T, lower=True).T
-    basis_two = jax.scipy.linalg.solve_triangular(tri_two, resid[:, P_SIZE:].T, lower=True).T
-    inner = jnp.dot(tri_one.T, coef[512:, P_SIZE:], precision=lax.Precision.HIGHEST)
-    new_basis = jnp.concatenate([basis_one, basis_two], axis=1) * scale_rows
-    upper = jnp.concatenate([tri_one.T, inner], axis=1)
-    lower = jnp.concatenate([jnp.zeros((P_SIZE, P_SIZE), F32), tri_two.T], axis=1)
-    return new_basis, jnp.concatenate([coef[:512], upper, lower], axis=0)
+    scale = math.sqrt(prior_basis.shape[0] * 256)
+    return finish(scale, sum_small(small), coef, resid)
 
 
 def solution(mesh):

time: 152 us -> 127 us (0.84)
  other arithmetic: 27.2 us -> 1.15 us
  Pallas kernels: 118 us -> 122 us
  matrix products: 1.63 us -> 0 us
    another operation x8 -> x0, other arithmetic: 23 us -> none  [the longest x3 6.68 us: shards(): tri_one = jnp.linalg.cholesky(grams[:, :P_SIZE])]
    pallas_call x0 -> x1, Pallas kernels: none -> 3.89 us  [finish(): pl.pallas_call(functools.partial(finish_kernel, scale), out_shape=(jax.Sh...]
where the time goes in v2:
time: 127 us
  Pallas kernels  122 us (96%)
  between operations  2.17 us (2%)
  local copies, waits for them, and re-layouts  2.08 us (2%)
    pallas_call x1, Pallas kernels, sketch_gram(): pl.pallas_call(gram_kernel, out_shape=jax.ShapeDtypeStruct((640, 640), F3...  75.2 us
    pallas_call x1, Pallas kernels, solve(): pl.pallas_call(solve_kernel, out_shape=(jax.ShapeDtypeStruct((576, 128),...  22.6 us
    pallas_call x1, Pallas kernels, sum_small(): pl.pallas_call(sum_kernel, out_shape=jax.ShapeDtypeStruct((64, 128), F32)...  20 us
    pallas_call x1, Pallas kernels, finish(): pl.pallas_call(functools.partial(finish_kernel, scale), out_shape=(jax.Sh...  3.89 us

profile of v2, /device:TPU:1, one launch (start us, length us, event | category | flops | bytes accessed | tf_op | source)
XLA Modules:
  0.0 127.2 jit_solution(4237416976854212655)
XLA Ops:
  0.6 0.0 copy-start
  0.6 0.0 copy-start.1
  2.1 0.0 copy-done
  2.1 0.1 constant_dynamic-slice_fusion
  2.2 1.1 broadcast_multiply_fusion
  3.4 0.0 copy-done.1
  3.4 75.2 %sketch_gram.1.gram = f32[640,640]{1,0:T(8,128)S(1)} custom-call(f32[2048,256]{1,0:T(8,128)S(1)} %copy-done.1, f32[256,640]{1,0:T(8,128)S(1)} %pad_maximum_fusion.wide), custom_call_target="tpu_custom_call" | custom-call | tf_op jit(solution)/shard_map/sketch_gram/pallas_call | solution.py:236
  78.6 22.6 %solve.1 = (f32[576,128]{1,0:T(8,128)S(1)}, f32[256,128]{1,0:T(8,128)S(1)}, f32[64,128]{1,0:T(8,128)S(1)}) custom-call(s32[1]{0:T(128)} %copy.8.count, f32[640,640]{1,0:T(8,128)S(1)} %sketch_gram.1.gram, f32[256,640]{1,0:T(8,128)S(1)} %pad_maximum_fusion.wide), custom_call_target="tpu_custom_call" | custom-call | tf_op jit(solution)/shard_map/solve/pallas_call | solution.py:311
  101.3 0.0 copy-start.2
  101.3 0.7 copy-done.2
  102.0 0.0 copy-start.3
  102.0 0.6 copy-done.3
  102.6 0.0 copy-start.4
  102.7 0.6 copy-done.4
  103.3 20.0 %sum_small.1.small = f32[64,128]{1,0:T(8,128)} custom-call(f32[64,128]{1,0:T(8,128)} %copy-done.4), custom_call_target="tpu_custom_call" | custom-call | tf_op jit(solution)/shard_map/sum_small/pallas_call | solution.py:384
  123.3 3.9 %finish.1 = (f32[256,128]{1,0:T(8,128)}, f32[640,128]{1,0:T(8,128)}) custom-call(f32[64,128]{1,0:T(8,128)} %sum_small.1.small, f32[576,128]{1,0:T(8,128)} %copy-done.2, f32[256,128]{1,0:T(8,128)} %copy-done.3), custom_call_target="tpu_custom_call" | custom-call | tf_op jit(solution)/shard_map/finish/pallas_call | solution.py:450
  (2 shorter events, 0.1 us)
Async XLA Ops:
  0.6 1.5 %copy-start = (f32[256,256]{1,0:T(8,128)S(1)}, f32[256,256]{1,0:T(8,128)}, u32[]{:S(2)}) copy-start(f32[256,256]{1,0:T(8,128)} %param.7) | copy-start | bytes 786436
  0.6 2.8 %copy-start.1 = (f32[2048,256]{1,0:T(8,128)S(1)}, f32[2048,256]{1,0:T(8,128)}, u32[]{:S(2)}) copy-start(f32[2048,256]{1,0:T(8,128)} %sketch.1) | copy-start | bytes 6291460
  101.3 0.7 copy-start.2
  102.0 0.7 copy-start.3
  102.6 0.6 copy-start.4

commit v3 on v0

v3 whole, which is shorter than its diff:
```python
import functools
import math

import jax
import jax.numpy as jnp
from jax import lax
from jax.experimental import pallas as pl
from jax.experimental.pallas import tpu as pltpu
from jax.sharding import Mesh
from jax.sharding import PartitionSpec as P

P_SIZE = 64
AXES = ("x", "z", "y", "c")
MESH = pl.DeviceIdType.MESH
F32 = jnp.float32
BF16 = jnp.bfloat16


def vmem():
    return pl.BlockSpec(memory_space=pltpu.VMEM)


def dot(left, right):
    return jnp.dot(left, right, precision=lax.Precision.HIGHEST, preferred_element_type=F32)


def dot_rows(left, right):
    return lax.dot_general(
        left, right, (((0,), (0,)), ((), ())), precision=lax.Precision.HIGHEST, preferred_element_type=F32
    )


def split(value):
    high = value.astype(BF16)
    return high, (value - high.astype(F32)).astype(BF16)


def halves(place):
    first = (place + 1) - 2 * lax.rem(place, 2)
    second = lax.rem(place + 3 + 2 * lax.rem(place, 2), 4)
    return (first, lax.rem((place + 1) // 2, 2)), (second, place // 2)


def square(part_high, part_low, lo):
    value = None
    for left in (part_low, part_high):
        for right in (part_low, part_high):
            term = lax.dot_general(
                left[:, lo:lo + 128], right[:, lo:], (((0,), (0,)), ((), ())), preferred_element_type=F32
            )
            value = term if value is None else value + term
    return value


def choose(panel, index):
    return jnp.where(
        index == 0, panel[:, 0:128], jnp.where(index == 1, panel[:, 64:192], panel[:, 128:256])
    )


ARRIVALS = (0, 1, 7, 2, 6, 3, 5, 4)
BLOCKS = [(i, j) for i in range(5) for j in range(i, 5)]
TILE = (8, 768)
NEAREST_FIRST = (1, 7, 2, 6, 3, 5, 4)


def gram_kernel(count, index, sketch_hbm, prior_hbm, panel_hbm, out, plain, sketch, prior, panel, high, low, dense, away, came, acc,
                r0, r1, r2, r3, zout, zin, zall, full, mine, other, load,
                d_send, d_recv, r_send, r_recv, z_send, z_recv, y_send, y_recv, a_send, a_recv, m_send, m_recv, b_send, b_recv):
    loads = [pltpu.make_async_copy(prior_hbm, prior, load.at[0]), pltpu.make_async_copy(panel_hbm, panel, load.at[1])]
    for i in range(8):
        rows = pl.ds(256 * i, 256)
        loads.append(pltpu.make_async_copy(sketch_hbm.at[rows], sketch.at[rows], load.at[2 + i]))
    for copy in loads:
        copy.start()

    x, z, y, c = (lax.axis_index(name) for name in AXES)
    (xa, xa_bit), (xb, xb_bit) = halves(x)
    (ya, ya_bit), (yb, yb_bit) = halves(y)
    bits = (xa_bit, ya_bit, xb_bit, yb_bit)
    links = ({"x": xa}, {"y": ya}, {"x": xb}, {"y": yb})
    ring = [{"z": lax.rem(z + step, 8)} for step in range(1, 8)]
    peer = {"c": 1 - c}

    barrier = pltpu.get_barrier_semaphore()
    for target in [peer] + list(links) + ring:
        pl.semaphore_signal(barrier, inc=1, device_id=target, device_id_type=MESH)

    def remote(source, target, send, recv, device):
        return pltpu.make_async_remote_copy(
            src_ref=source, dst_ref=target, send_sem=send, recv_sem=recv, device_id=device, device_id_type=MESH
        )

    def kept(s, t, bits=bits):
        return sum([bits[(s + u) % 4] * (8 >> u) for u in range(t)], jnp.int32(0))

    def gone(s, t, bits=bits):
        return kept(s, t, bits) + (1 - bits[(s + t) % 4]) * (8 >> t)

    turned_bits, turned_links = [], []
    for turn in range(4):
        link = lax.rem(z + turn, 4)
        upper, odd = link // 2, lax.rem(link, 2)

        def pick(values):
            return (1 - upper) * ((1 - odd) * values[0] + odd * values[1]) + upper * (
                (1 - odd) * values[2] + odd * values[3]
            )

        turned_bits.append(pick(bits))
        turned_links.append({"x": pick((xa, x, xb, x)), "y": pick((y, ya, y, yb))})

    for copy in loads[:2]:
        copy.wait()
    keep = lax.broadcasted_iota(jnp.int32, (256, 512), 1) < count[0]
    high[:, :512], low[:, :512] = split(jnp.where(keep, prior[...], 0.0))
    high[:, 512:], low[:, 512:] = split(choose(panel, index[0]))
    for i in range(5):
        lo = 128 * i
        value = square(high, low, lo)
        for j in range(i, 5):
            at = 128 * (j - i)
            dense[BLOCKS.index((i, j))] = value[:, at:at + 128].reshape(16, 8, 128)
    dense[15] = jnp.zeros((16, 8, 128), F32)
    for copy in loads[2:]:
        copy.wait()

    def product(core, tiles, target):
        rows = [sketch[pl.ds(pl.multiple_of(core * 1024 + s * 128 + tiles[s] * 8, 64), 64), :] for s in range(8)]
        part_high, part_low = split(jnp.concatenate(rows, axis=0))
        value = jnp.dot(part_high, low[...], preferred_element_type=F32)
        value = value + jnp.dot(part_low, high[...], preferred_element_type=F32)
        value = value + jnp.dot(part_high, high[...], preferred_element_type=F32)
        for s in range(8):
            target[s, pl.ds(tiles[s], 8), :, :640] = value[64 * s:64 * s + 64].reshape(8, 8, 640)
            target[s, pl.ds(tiles[s], 8), :, 640:] = dense[core * 8 + s, pl.ds(tiles[s], 8)]

    parts = ([gone(s, 0) for s in range(8)], [kept(s, 1) for s in range(8)])

    def chunk(part, s):
        tile = parts[part][s]
        return remote(
            away.at[s, pl.ds(tile, 8)], came.at[s, pl.ds(tile, 8)], d_send.at[part, s], d_recv.at[part, s], peer
        )

    for part in range(2):
        product(1 - c, parts[part], away)
    product(c, parts[0], acc)
    pl.semaphore_wait(barrier, 12)
    for part in range(2):
        for s in range(8):
            chunk(part, s).start()
    product(c, parts[1], acc)

    landing = (r0, r1, r2, r3)

    def scatter(t, s):
        size = 8 >> t
        return remote(
            acc.at[s, pl.ds(gone(s, t), size)], landing[t].at[s], r_send.at[t, s], r_recv.at[t, s],
            links[(s + t) % 4],
        )

    def along(s):
        return remote(zout.at[s], zin.at[z], z_send.at[s], z_recv.at[z], {"z": jnp.int32(s)})

    for part in range(2):
        for s in range(8):
            chunk(part, s).wait_recv()
            acc[s, pl.ds(parts[part][s], 8)] += came[s, pl.ds(parts[part][s], 8)]
            if part == 0:
                scatter(0, s).start()
    for t in range(4):
        size = 8 >> t
        for s in range(8):
            scatter(t, s).wait_recv()
            at = kept(s, t + 1)
            if t < 3:
                acc[s, pl.ds(at, size)] += landing[t][s]
                scatter(t + 1, s).start()
            else:
                zout[pl.ds(s, 1)] = acc[s, pl.ds(at, 1)] + r3[s]

                @pl.when(z != s)
                def _():
                    along(s).start()

    total = zout[z]
    for step in range(1, 8):
        source = lax.rem(z + step, 8)
        remote(zout.at[0], zin.at[source], z_send.at[0], z_recv.at[source], ring[0]).wait_recv()
        total = total + zin[source]
    zall[0] = total

    def back(step):
        return remote(zall.at[0], zall.at[8 - step], y_send.at[step - 1], y_recv.at[step - 1], ring[step - 1])

    for step in NEAREST_FIRST:
        back(step).start()

    def gather(t, s):
        here = full.at[s, pl.ds(kept(s, t + 1, turned_bits), 8 >> t)]
        source = zall.at[pl.ds(s, 1)] if t == 3 else here
        return remote(source, here, a_send.at[t, s], a_recv.at[t, s], turned_links[(s + t) % 4])

    for s in ARRIVALS:
        if s:
            back(8 - s).wait_recv()
        gather(3, s).start()
        full[s, pl.ds(kept(s, 4, turned_bits), 1)] = zall[pl.ds(s, 1)]
    for t in (3, 2, 1):
        for s in ARRIVALS:
            gather(t, s).wait_recv()
            gather(t - 1, s).start()

    def swap(i):
        lo = 128 * i
        place = (pl.ds(lo, 128), pl.ds(lo, 640 - lo))
        return remote(mine.at[place], other.at[place], m_send.at[i], m_recv.at[i], peer)

    ours = pl.ds(8 * c, 8)
    trade = remote(plain.at[ours], plain.at[ours], b_send, b_recv, peer)

    def add_gram(rows, first, last):
        part_high, part_low = split(rows)
        for i in range(5):
            lo = 128 * i
            value = square(part_high, part_low, lo)
            if first:
                mine[lo:lo + 128, lo:] = value
            else:
                mine[lo:lo + 128, lo:] += value
            if last:
                swap(i).start()

    def part_of(s, at):
        return full[s, pl.ds(at, 8), :, :640].reshape(64, 640)

    add_gram(jnp.concatenate([part_of(s, kept(s, 1, turned_bits)) for s in range(8)], axis=0), True, False)
    for last, some in ((False, ARRIVALS[:4]), (True, ARRIVALS[4:])):
        rows = []
        for s in some:
            gather(0, s).wait_recv()
            rows.append(part_of(s, gone(s, 0, turned_bits)))
            plain[8 * c + lax.rem(z + s, 8)] = full[s, :, :, 640:]
        if last:
            trade.start()
        add_gram(jnp.concatenate(rows, axis=0), False, last)
    for i in range(5):
        lo = 128 * i
        swap(i).wait_recv()
        out[lo:lo + 128, lo:] = mine[lo:lo + 128, lo:] + other[lo:lo + 128, lo:]
    trade.wait_recv()

    for s in range(8):
        for part in range(2):
            chunk(part, s).wait_send()
        for t in range(4):
            scatter(t, s).wait_send()
            gather(t, s).wait_send()

        @pl.when(z != s)
        def _():
            along(s).wait_send()

    for step in range(1, 8):
        back(step).wait_send()
    for i in range(5):
        swap(i).wait_send()
    trade.wait_send()


def sketch_gram(count, index, sketch, prior, panel):
    dma = pltpu.SemaphoreType.DMA
    stream = (8, 16) + TILE
    scratch = [pltpu.VMEM((2048, 256), F32), pltpu.VMEM((256, 512), F32), pltpu.VMEM((256, 256), F32)]
    scratch += [pltpu.VMEM((256, 640), BF16)] * 2 + [pltpu.VMEM((16, 16, 8, 128), F32)]
    scratch += [pltpu.VMEM(stream, F32)] * 3
    scratch += [pltpu.VMEM((8, 8 >> t) + TILE, F32) for t in range(4)]
    scratch += [pltpu.VMEM((8,) + TILE, F32)] * 3
    scratch += [pltpu.VMEM(stream, F32)]
    scratch += [pltpu.VMEM((640, 640), F32)] * 2
    scratch += [dma((10,))] + [dma((2, 8))] * 2 + [dma((4, 8))] * 2
    scratch += [dma((8,))] * 2 + [dma((7,))] * 2 + [dma((4, 8))] * 2 + [dma((5,))] * 2 + [dma] * 2
    smem = pl.BlockSpec(memory_space=pltpu.SMEM)
    hbm = pl.BlockSpec(memory_space=pl.ANY)
    return pl.pallas_call(
        gram_kernel,
        out_shape=(jax.ShapeDtypeStruct((640, 640), F32), jax.ShapeDtypeStruct((16, 16, 8, 128), F32)),
        in_specs=[smem, smem, hbm, hbm, hbm],
        out_specs=(vmem(),) * 2,
        scratch_shapes=scratch,
        compiler_params=pltpu.CompilerParams(
            collective_id=0, has_side_effects=True, vmem_limit_bytes=56 * 1024 * 1024
        ),
        name="sketch_gram",
    )(count, index, sketch, prior, panel)


def sweep(blocks, panels):
    blocks = list(blocks)
    lane = lax.broadcasted_iota(jnp.int32, (8, 128), 1)
    row = lax.broadcasted_iota(jnp.int32, (8, 128), 0)
    for p in range(panels):
        k = 8 * p
        inside = (lane >= k) & (lane < k + 8)
        cols = [[jnp.broadcast_to(b[:, k + s:k + s + 1], (8, 128)) for s in range(8)] for b in blocks]
        e = list(cols[p])
        r = jnp.where(inside, (lane - k == row).astype(F32), blocks[p])
        for s in range(8):
            inv = 1.0 / e[s][s:s + 1, :]
            rs = r[s:s + 1, :] * inv
            r = jnp.where(row == s, rs, r - e[s] * rs)
            for u in range(s + 1, 8):
                es = e[u][s:s + 1, :] * inv
                e[u] = jnp.where(row == s, es, e[u] - e[s] * es)
        rows = [r[s:s + 1, :] for s in range(8)]
        for i in range(len(blocks)):
            if i == p:
                continue
            total = jnp.where(inside, 0.0, blocks[i])
            for s in range(8):
                total = total - cols[i][s] * rows[s]
            blocks[i] = total
        blocks[p] = r
    return blocks


def factor(small):
    lane = lax.broadcasted_iota(jnp.int32, (8, 128), 1)
    row = lax.broadcasted_iota(jnp.int32, (8, 128), 0)
    left = lane < P_SIZE
    place = jnp.where(left, lane, lane - P_SIZE)
    blocks = [small[8 * i:8 * i + 8, :] for i in range(8)]
    extra = [(place == row + 8 * i).astype(F32) for i in range(8)]
    roots, inverses = [], []
    for p in range(8):
        k = 8 * p

        def column(block, s):
            first = jnp.broadcast_to(block[:, k + s:k + s + 1], (8, 128))
            second = jnp.broadcast_to(block[:, P_SIZE + k + s:P_SIZE + k + s + 1], (8, 128))
            return jnp.where(left, first, second)

        cols = {i: [column(blocks[i], s) for s in range(8)] for i in range(p, 8)}
        e = list(cols[p])
        r, q = blocks[p], extra[p]
        for s in range(8):
            pivot = e[s][s:s + 1, :]
            inv = 1.0 / pivot
            root = lax.rsqrt(pivot)
            roots.append(jnp.where(place[:1] >= k + s, r[s:s + 1, :] * root, 0.0))
            inverses.append(q[s:s + 1, :] * root)
            rs, qs = r[s:s + 1, :] * inv, q[s:s + 1, :] * inv
            here = row == s
            r = jnp.where(here, rs, r - e[s] * rs)
            q = jnp.where(here, qs, q - e[s] * qs)
            for u in range(s + 1, 8):
                es = e[u][s:s + 1, :] * inv
                e[u] = jnp.where(here, es, e[u] - e[s] * es)
        for i in range(p + 1, 8):
            for s in range(8):
                blocks[i] = blocks[i] - cols[i][s] * r[s:s + 1, :]
                extra[i] = extra[i] - cols[i][s] * q[s:s + 1, :]
    return jnp.concatenate(roots, axis=0), jnp.concatenate(inverses, axis=0)


def project_kernel(scale, count, index, gram, plain, prior, panel, basis, factors, a, b):
    r = lax.broadcasted_iota(jnp.int32, (128, 128), 0)
    c = lax.broadcasted_iota(jnp.int32, (128, 128), 1)
    on_left = lax.broadcasted_iota(jnp.int32, (64, 128), 1) < P_SIZE
    for at, (i, j) in enumerate(BLOCKS):
        block = plain[at].reshape(128, 128)
        b[128 * i:128 * i + 128, 128 * j:128 * j + 128] = block
        if i != j:
            b[128 * j:128 * j + 128, 128 * i:128 * i + 128] = block.T
    for i in range(5):
        a[128 * i:128 * i + 128, 128 * i:] = gram[128 * i:128 * i + 128, 128 * i:]
    for k in range(4):
        lo = 128 * k
        hi = lo + 128
        unused = (c + lo >= count[0]) & (r == c)
        block = a[lo:hi, lo:hi] + jnp.where(unused, 1.0, 0.0)
        inverse = jnp.concatenate(sweep([block[8 * i:8 * i + 8] for i in range(16)], 16), axis=0)
        y = dot(inverse, a[lo:hi, hi:])
        for i in range(k + 1, 5):
            left = 128 * i
            a[left:left + 128, left:] -= dot_rows(a[lo:hi, left:left + 128], y[:, left - hi:])
        if k:
            a[:lo, hi:] -= dot(a[:lo, lo:hi], y)
        a[lo:hi, hi:] = y
    coefs = a[:512, 512:]
    tail = a[512:, 512:]
    both = jnp.concatenate(sweep([tail[8 * i:8 * i + 8] for i in range(8)], 8), axis=0)
    ratio = jnp.where(on_left, 0.0, both)
    ends = (r == c).astype(F32) - jnp.concatenate([ratio, jnp.zeros((64, 128), F32)], axis=0)
    weights = jnp.concatenate([dot(coefs[:, :P_SIZE], ratio) - coefs, ends], axis=0)
    own = dot_rows(weights, dot(b[...], weights))
    small = jnp.concatenate([own[:P_SIZE, :P_SIZE], own[P_SIZE:, P_SIZE:]], axis=1)
    keep = lax.broadcasted_iota(jnp.int32, (256, 512), 1) < count[0]
    resid = choose(panel, index[0]) - dot(jnp.where(keep, prior[...], 0.0), coefs)
    resid = resid - dot(resid[:, :P_SIZE], ratio)
    tri, inverse = factor(small)
    both = jnp.concatenate([jnp.where(on_left, inverse, 0.0), jnp.where(on_left, 0.0, inverse)], axis=0)
    basis[...] = scale * lax.dot_general(
        resid, both, (((1,), (1,)), ((), ())), precision=lax.Precision.HIGHEST, preferred_element_type=F32
    )
    tri_one = jnp.where(on_left, tri, 0.0)
    factors[0:512, :] = coefs
    factors[512:576, :] = tri_one + dot(tri_one[:, :P_SIZE], ratio)
    factors[576:640, :] = jnp.where(on_left, 0.0, tri)


def project(scale, count, index, gram, plain, prior, panel):
    return pl.pallas_call(
        functools.partial(project_kernel, scale),
        out_shape=(jax.ShapeDtypeStruct((256, 128), F32), jax.ShapeDtypeStruct((640, 128), F32)),
        in_specs=[pl.BlockSpec(memory_space=pltpu.SMEM)] * 2 + [vmem()] * 4,
        out_specs=(vmem(),) * 2,
        scratch_shapes=[pltpu.VMEM((640, 640), F32)] * 2,
        compiler_params=pltpu.CompilerParams(vmem_limit_bytes=32 * 1024 * 1024),
        name="project",
    )(count, index, gram, plain, prior, panel)


def shards(sketch, prior_basis, panel_block, panel_index, prior_count):
    gram, plain = sketch_gram(prior_count, panel_index, sketch, prior_basis, panel_block)
    scale = math.sqrt(prior_basis.shape[0] * 256)
    return project(scale, prior_count, panel_index, gram, plain, prior_basis, panel_block)


def solution(mesh):
    torus = Mesh(mesh.devices.reshape(4, 8, 4, 2), AXES)
    return jax.shard_map(
        shards,
        mesh=torus,
        in_specs=(P(None, AXES), P(AXES, None), P(AXES, None), P(), P()),
        out_specs=(P(AXES, None), P()),
        check_vma=False,
    )
```

time: 672 us -> 105 us (0.16); the launches traced: 664 us -> 105 us
  waiting for transfers between devices: 274 us -> 0 us
  other arithmetic: 162 us -> 0 us
  blocking collectives: 127 us -> 0 us
  Pallas kernels: 0 us -> 99.9 us
  matrix products: 62 us -> 0 us
  local copies, waits for them, and re-layouts: 20.1 us -> 2.66 us
  between operations: 19.3 us -> 2.04 us
    psum x1 -> x0, waiting for transfers between devices: 274 us -> none  [shards(): prior_sketch = lax.psum(local_prior, ROWS_GRP)]
    another operation x31 -> x0, other arithmetic: 157 us -> none  [the longest x14 79 us: shards(): prior_factor = jnp.linalg.cholesky(gram_prior)]
    psum x8 -> x0, blocking collectives: 127 us -> none  [by_axis(): return functools.reduce(lax.psum, axes, value)]
    pallas_call x0 -> x2, Pallas kernels: none -> 99.9 us  [the longest x1 72.7 us: sketch_gram(): pl.pallas_call(gram_kernel, out_shape=(jax.ShapeDtypeStruct((640, 640), F...]
    dot_general x14 -> x0, matrix products: 44.9 us -> none  [matmul(): return jnp.dot(left, right, precision=lax.Precision.HIGHEST)]
    another operation x39 -> x0, matrix products: 17.2 us -> none  [the longest x28 7.65 us: shards(): jax.scipy.linalg.cho_solve((prior_factor, True), matmul(prior_sketch.T, s...]
    another operation x18 -> x0, local copies, waits for them, and re-layouts: 11 us -> none  [the longest x13 10.7 us: shards(): jax.scipy.linalg.cho_solve((prior_factor, True), matmul(prior_sketch.T, s...]
  transfers between devices with their start and end apart: 1 -> 0, of which waited for: 1 -> 0; matrix products, arithmetic and copies ran while one was open for 0% -> 0% of each run, Pallas kernels for 0% -> 0%
where the time goes in v3:
time: 105 us
  Pallas kernels  99.9 us (95%)
  local copies, waits for them, and re-layouts  2.66 us (3%)
  between operations  2.04 us (2%)
    pallas_call x1, Pallas kernels, sketch_gram(): pl.pallas_call(gram_kernel, out_shape=(jax.ShapeDtypeStruct((640, 640), F...  72.7 us
    pallas_call x1, Pallas kernels, project(): pl.pallas_call(functools.partial(project_kernel, scale), out_shape=(jax.S...  27.2 us
    unnamed x8, local copies, waits for them, and re-layouts  2.66 us

profile of v3, /device:TPU:1, one launch (start us, length us, event | category | flops | bytes accessed | tf_op | source)
XLA Modules:
  0.0 104.6 jit_solution(12992794438230123037)
XLA Ops:
  0.6 0.0 copy-start.3
  0.6 0.0 copy-start
  2.0 72.7 %sketch_gram.1 = (f32[640,640]{1,0:T(8,128)}, f32[16,16,8,128]{3,2,1,0:T(8,128)}) custom-call(s32[1]{0:T(128)S(6)} %copy.8.count, s32[1]{0:T(128)S(6)} %copy.7.index, f32[2048,256]{1,0:T(8,128)} %sketch_hbm.1, f32[256,512]{1,0:T(8,128)} %prior.1, f32[256,256]{1,0:T(8,128)} %panel.1), custom_call_target="tpu_custom_call" | custom-call | tf_op jit(solution)/shard_map/sketch_gram/pallas_call | solution.py:287
  74.7 0.0 copy-done.3
  74.7 0.0 copy-done
  74.7 0.0 copy-start.1
  74.7 1.4 %copy-done.1 = f32[640,640]{1,0:T(8,128)S(1)} copy-done((f32[640,640]{1,0:T(8,128)S(1)}, f32[640,640]{1,0:T(8,128)}, u32[]{:S(2)}) %copy-start.1) | copy-done | bytes 1638424
  76.1 0.0 copy-start.2
  76.1 1.2 %copy-done.2 = f32[16,16,8,128]{3,2,1,0:T(8,128)S(1)} copy-done((f32[16,16,8,128]{3,2,1,0:T(8,128)S(1)}, f32[16,16,8,128]{3,2,1,0:T(8,128)}, u32[]{:S(2)}) %copy-start.2) | copy-done | bytes 1048600
  77.4 27.2 %project.1 = (f32[256,128]{1,0:T(8,128)}, f32[640,128]{1,0:T(8,128)}) custom-call(s32[1]{0:T(128)S(6)} %copy.8.count, s32[1]{0:T(128)S(6)} %copy.7.index, f32[640,640]{1,0:T(8,128)S(1)} %copy-done.1, f32[16,16,8,128]{3,2,1,0:T(8,128)S(1)} %copy-done.2, f32[256,512]{1,0:T(8,128)S(1)} %copy-done, f32[256,256]{1,0:T(8,128)S(1)} %copy-done.3), custom_call_target="tpu_custom_call" | custom-call | tf_op jit(solution)/shard_map/project/pallas_call | solution.py:415
Async XLA Ops:
  0.6 74.1 %copy-start.3 = (f32[256,256]{1,0:T(8,128)S(1)}, f32[256,256]{1,0:T(8,128)}, u32[]{:S(2)}) copy-start(f32[256,256]{1,0:T(8,128)} %panel.1) | copy-start | bytes 786436
  0.6 74.1 %copy-start = (f32[256,512]{1,0:T(8,128)S(1)}, f32[256,512]{1,0:T(8,128)}, u32[]{:S(2)}) copy-start(f32[256,512]{1,0:T(8,128)} %prior.1) | copy-start | bytes 1572868
  74.7 1.4 %copy-start.1 = (f32[640,640]{1,0:T(8,128)S(1)}, f32[640,640]{1,0:T(8,128)}, u32[]{:S(2)}) copy-start(f32[640,640]{1,0:T(8,128)} %get-tuple-element.4.gram) | copy-start | bytes 4915204
  76.1 1.2 %copy-start.2 = (f32[16,16,8,128]{3,2,1,0:T(8,128)S(1)}, f32[16,16,8,128]{3,2,1,0:T(8,128)}, u32[]{:S(2)}) copy-start(f32[16,16,8,128]{3,2,1,0:T(8,128)} %get-tuple-element.5.plain) | copy-start | bytes 3145732

commit v4 on v3

--- a/solution.py
+++ b/solution.py
@@ -65,7 +65,7 @@
 
 
 def gram_kernel(count, index, sketch_hbm, prior_hbm, panel_hbm, out, plain, sketch, prior, panel, high, low, dense, away, came, acc,
-                r0, r1, r2, r3, zout, zin, zall, full, mine, other, load,
+                r0, r1, r2, zout, zin, zall, full, mine, other, load,
                 d_send, d_recv, r_send, r_recv, z_send, z_recv, y_send, y_recv, a_send, a_recv, m_send, m_recv, b_send, b_recv):
     loads = [pltpu.make_async_copy(prior_hbm, prior, load.at[0]), pltpu.make_async_copy(panel_hbm, panel, load.at[1])]
     for i in range(8):
@@ -83,7 +83,8 @@
     peer = {"c": 1 - c}
 
     barrier = pltpu.get_barrier_semaphore()
-    for target in [peer] + list(links) + ring:
+    corners = [{**links[i], **links[(i + 1) % 4]} for i in range(4)]
+    for target in [peer] + list(links) + corners + ring:
         pl.semaphore_signal(barrier, inc=1, device_id=target, device_id_type=MESH)
 
     def remote(source, target, send, recv, device):
@@ -146,13 +147,13 @@
     for part in range(2):
         product(1 - c, parts[part], away)
     product(c, parts[0], acc)
-    pl.semaphore_wait(barrier, 12)
+    pl.semaphore_wait(barrier, 16)
     for part in range(2):
         for s in range(8):
             chunk(part, s).start()
     product(c, parts[1], acc)
 
-    landing = (r0, r1, r2, r3)
+    landing = (r0, r1)
 
     def scatter(t, s):
         size = 8 >> t
@@ -161,6 +162,16 @@
             links[(s + t) % 4],
         )
 
+    def corner(s, slot):
+        over, up = bits[(s + 2) % 4], bits[(s + 3) % 4]
+        over = over if slot == 1 else 1 - over
+        up = up if slot == 0 else 1 - up
+        device = (links[(s + 2) % 4], links[(s + 3) % 4], corners[(s + 2) % 4])[slot]
+        return remote(
+            acc.at[s, pl.ds(kept(s, 2) + 2 * over + up, 1)], r2.at[s, pl.ds(slot, 1)],
+            r_send.at[2 + slot, s], r_recv.at[2 + slot, s], device,
+        )
+
     def along(s):
         return remote(zout.at[s], zin.at[z], z_send.at[s], z_recv.at[z], {"z": jnp.int32(s)})
 
@@ -170,20 +181,24 @@
             acc[s, pl.ds(parts[part][s], 8)] += came[s, pl.ds(parts[part][s], 8)]
             if part == 0:
                 scatter(0, s).start()
-    for t in range(4):
+    for t in range(2):
         size = 8 >> t
         for s in range(8):
             scatter(t, s).wait_recv()
-            at = kept(s, t + 1)
-            if t < 3:
-                acc[s, pl.ds(at, size)] += landing[t][s]
-                scatter(t + 1, s).start()
+            acc[s, pl.ds(kept(s, t + 1), size)] += landing[t][s]
+            if t == 0:
+                scatter(1, s).start()
             else:
-                zout[pl.ds(s, 1)] = acc[s, pl.ds(at, 1)] + r3[s]
-
-                @pl.when(z != s)
-                def _():
-                    along(s).start()
+                for slot in (2, 0, 1):
+                    corner(s, slot).start()
+    for s in range(8):
+        for slot in range(3):
+            corner(s, slot).wait_recv()
+        zout[s] = acc[s, kept(s, 4)] + (r2[s, 0] + r2[s, 1] + r2[s, 2])
+
+        @pl.when(z != s)
+        def _():
+            along(s).start()
 
     total = zout[z]
     for step in range(1, 8):
@@ -200,18 +215,27 @@
 
     def gather(t, s):
         here = full.at[s, pl.ds(kept(s, t + 1, turned_bits), 8 >> t)]
-        source = zall.at[pl.ds(s, 1)] if t == 3 else here
-        return remote(source, here, a_send.at[t, s], a_recv.at[t, s], turned_links[(s + t) % 4])
+        return remote(here, here, a_send.at[t, s], a_recv.at[t, s], turned_links[(s + t) % 4])
+
+    def gather_corner(s, slot):
+        one, two = turned_links[(s + 2) % 4], turned_links[(s + 3) % 4]
+        device = (one, two, {"x": one["x"] + two["x"] - x, "y": one["y"] + two["y"] - y})[slot]
+        here = full.at[s, pl.ds(kept(s, 4, turned_bits), 1)]
+        return remote(zall.at[pl.ds(s, 1)], here, a_send.at[2 + slot, s], a_recv.at[2 + slot, s], device)
 
     for s in ARRIVALS:
         if s:
             back(8 - s).wait_recv()
-        gather(3, s).start()
+        for slot in (2, 0, 1):
+            gather_corner(s, slot).start()
         full[s, pl.ds(kept(s, 4, turned_bits), 1)] = zall[pl.ds(s, 1)]
-    for t in (3, 2, 1):
-        for s in ARRIVALS:
-            gather(t, s).wait_recv()
-            gather(t - 1, s).start()
+    for s in ARRIVALS:
+        for slot in range(3):
+            gather_corner(s, slot).wait_recv()
+        gather(1, s).start()
+    for s in ARRIVALS:
+        gather(1, s).wait_recv()
+        gather(0, s).start()
 
     def swap(i):
         lo = 128 * i
@@ -255,9 +279,12 @@
     for s in range(8):
         for part in range(2):
             chunk(part, s).wait_send()
-        for t in range(4):
+        for t in range(2):
             scatter(t, s).wait_send()
             gather(t, s).wait_send()
+        for slot in range(3):
+            corner(s, slot).wait_send()
+            gather_corner(s, slot).wait_send()
 
         @pl.when(z != s)
         def _():
@@ -276,14 +303,14 @@
     scratch = [pltpu.VMEM((2048, 256), F32), pltpu.VMEM((256, 512), F32), pltpu.VMEM((256, 256), F32)]
     scratch += [pltpu.VMEM((256, 640), BF16)] * 2 + [pltpu.VMEM((16, 16, 8, 128), F32)]
     scratch += [pltpu.VMEM(stream, F32)] * 3
-    scratch += [pltpu.VMEM((8, 8 >> t) + TILE, F32) for t in range(4)]
+    scratch += [pltpu.VMEM((8, size) + TILE, F32) for size in (8, 4, 3)]
     scratch += [pltpu.VMEM((8,) + TILE, F32)] * 3
     scratch += [pltpu.VMEM(stream, F32)]
     scratch += [pltpu.VMEM((640, 640), F32)] * 2
-    scratch += [dma((10,))] + [dma((2, 8))] * 2 + [dma((4, 8))] * 2
-    scratch += [dma((8,))] * 2 + [dma((7,))] * 2 + [dma((4, 8))] * 2 + [dma((5,))] * 2 + [dma] * 2
+    scratch += [dma((10,))] + [dma((2, 8))] * 2 + [dma((5, 8))] * 2
+    scratch += [dma((8,))] * 2 + [dma((7,))] * 2 + [dma((5, 8))] * 2 + [dma((5,))] * 2 + [dma] * 2
     smem = pl.BlockSpec(memory_space=pltpu.SMEM)
-    hbm = pl.BlockSpec(memory_space=pl.ANY)
+    hbm = pl.BlockSpec(memory_space=pltpu.MemorySpace.HBM)
     return pl.pallas_call(
         gram_kernel,
         out_shape=(jax.ShapeDtypeStruct((640, 640), F32), jax.ShapeDtypeStruct((16, 16, 8, 128), F32)),
@@ -291,39 +318,71 @@
         out_specs=(vmem(),) * 2,
         scratch_shapes=scratch,
         compiler_params=pltpu.CompilerParams(
-            collective_id=0, has_side_effects=True, vmem_limit_bytes=56 * 1024 * 1024
+            collective_id=0, has_side_effects=True, vmem_limit_bytes=50 * 1024 * 1024
         ),
         name="sketch_gram",
     )(count, index, sketch, prior, panel)
 
 
-def sweep(blocks, panels):
+def sweep(blocks, first):
+    panels = len(blocks)
     blocks = list(blocks)
     lane = lax.broadcasted_iota(jnp.int32, (8, 128), 1)
     row = lax.broadcasted_iota(jnp.int32, (8, 128), 0)
+
+    def columns(block, k):
+        return [jnp.broadcast_to(block[:, k + s:k + s + 1], (8, 128)) for s in range(8)]
+
+    e = columns(blocks[0], first)
     for p in range(panels):
-        k = 8 * p
+        k = first + 8 * p
         inside = (lane >= k) & (lane < k + 8)
-        cols = [[jnp.broadcast_to(b[:, k + s:k + s + 1], (8, 128)) for s in range(8)] for b in blocks]
-        e = list(cols[p])
+        cols = [columns(b, k) if i != p else None for i, b in enumerate(blocks)]
         r = jnp.where(inside, (lane - k == row).astype(F32), blocks[p])
-        for s in range(8):
+        more = p + 1 < panels
+        after = columns(blocks[p], k + 8) if more else []
+        following = columns(blocks[p + 1], k + 8) if more else []
+        for s in range(8):
+            here = row == s
             inv = 1.0 / e[s][s:s + 1, :]
-            rs = r[s:s + 1, :] * inv
-            r = jnp.where(row == s, rs, r - e[s] * rs)
+
+            def step(v):
+                own = v[s:s + 1, :] * inv
+                return jnp.where(here, own, v - e[s] * own)
+
             for u in range(s + 1, 8):
-                es = e[u][s:s + 1, :] * inv
-                e[u] = jnp.where(row == s, es, e[u] - e[s] * es)
-        rows = [r[s:s + 1, :] for s in range(8)]
+                e[u] = step(e[u])
+            after = [step(v) for v in after]
+            r = step(r)
+        if more:
+            e = []
+            for u in range(8):
+                terms = [cols[p + 1][s] * after[u][s:s + 1, :] for s in range(8)]
+                while len(terms) > 1:
+                    terms = [x + y for x, y in zip(terms[::2], terms[1::2])]
+                e.append(following[u] - terms[0])
         for i in range(len(blocks)):
             if i == p:
                 continue
             total = jnp.where(inside, 0.0, blocks[i])
             for s in range(8):
-                total = total - cols[i][s] * rows[s]
+                total = total - cols[i][s] * r[s:s + 1, :]
             blocks[i] = total
         blocks[p] = r
     return blocks
+
+
+def eliminated(rows, first):
+    return jnp.concatenate(sweep([rows[8 * i:8 * i + 8] for i in range(8)], first), axis=0)
+
+
+def inverse_of(block):
+    on_left = lax.broadcasted_iota(jnp.int32, (64, 128), 1) < P_SIZE
+    top = eliminated(block[:64], 0)
+    bottom = jnp.where(on_left, 0.0, block[64:]) - dot(block[64:, :64], top)
+    bottom = eliminated(bottom, 64)
+    top = jnp.where(on_left, top, 0.0) - dot(top[:, 64:], bottom)
+    return jnp.concatenate([top, bottom], axis=0)
 
 
 def factor(small):
@@ -381,8 +440,7 @@
         hi = lo + 128
         unused = (c + lo >= count[0]) & (r == c)
         block = a[lo:hi, lo:hi] + jnp.where(unused, 1.0, 0.0)
-        inverse = jnp.concatenate(sweep([block[8 * i:8 * i + 8] for i in range(16)], 16), axis=0)
-        y = dot(inverse, a[lo:hi, hi:])
+        y = dot(inverse_of(block), a[lo:hi, hi:])
         for i in range(k + 1, 5):
             left = 128 * i
             a[left:left + 128, left:] -= dot_rows(a[lo:hi, left:left + 128], y[:, left - hi:])
@@ -391,7 +449,7 @@
         a[lo:hi, hi:] = y
     coefs = a[:512, 512:]
     tail = a[512:, 512:]
-    both = jnp.concatenate(sweep([tail[8 * i:8 * i + 8] for i in range(8)], 8), axis=0)
+    both = eliminated(tail[:64], 0)
     ratio = jnp.where(on_left, 0.0, both)
     ends = (r == c).astype(F32) - jnp.concatenate([ratio, jnp.zeros((64, 128), F32)], axis=0)
     weights = jnp.concatenate([dot(coefs[:, :P_SIZE], ratio) - coefs, ends], axis=0)
@@ -418,13 +476,14 @@
         in_specs=[pl.BlockSpec(memory_space=pltpu.SMEM)] * 2 + [vmem()] * 4,
         out_specs=(vmem(),) * 2,
         scratch_shapes=[pltpu.VMEM((640, 640), F32)] * 2,
-        compiler_params=pltpu.CompilerParams(vmem_limit_bytes=32 * 1024 * 1024),
+        compiler_params=pltpu.CompilerParams(vmem_limit_bytes=16 * 1024 * 1024),
         name="project",
     )(count, index, gram, plain, prior, panel)
 
 
 def shards(sketch, prior_basis, panel_block, panel_index, prior_count):
-    gram, plain = sketch_gram(prior_count, panel_index, sketch, prior_basis, panel_block)
+    far = [pltpu.with_memory_space_constraint(v, pltpu.MemorySpace.HBM) for v in (sketch, prior_basis, panel_block)]
+    gram, plain = sketch_gram(prior_count, panel_index, *far)
     scale = math.sqrt(prior_basis.shape[0] * 256)
     return project(scale, prior_count, panel_index, gram, plain, prior_basis, panel_block)
 

time: 105 us -> 91.6 us (0.87)
  Pallas kernels: 99.9 us -> 89.5 us
  local copies, waits for them, and re-layouts: 2.66 us -> 0.01 us
    pallas_call x1, Pallas kernels: 27.2 us -> 21.5 us  [project(): pl.pallas_call(functools.partial(project_kernel, scale), out_shape=(jax.S...]
    pallas_call x1, Pallas kernels: 72.7 us -> 68 us  [sketch_gram(): pl.pallas_call(gram_kernel, out_shape=(jax.ShapeDtypeStruct((640, 640), F...]
    unnamed x8 -> x4, local copies, waits for them, and re-layouts: 2.66 us -> 0.01 us
where the time goes in v4:
time: 91.6 us; the launch traced here: 91.5 us
  Pallas kernels  89.5 us (98%)
  between operations  2.03 us (2%)
    pallas_call x1, Pallas kernels, sketch_gram(): pl.pallas_call(gram_kernel, out_shape=(jax.ShapeDtypeStruct((640, 640), F...  68 us
    pallas_call x1, Pallas kernels, project(): pl.pallas_call(functools.partial(project_kernel, scale), out_shape=(jax.S...  21.5 us

profile of v4, /device:TPU:1, one launch (start us, length us, event | category | flops | bytes accessed | tf_op | source)
XLA Modules:
  0.0 91.5 jit_solution(9761549918123056793)
XLA Ops:
  0.6 0.0 copy-start.1
  0.6 0.0 copy-start
  2.0 68.0 %sketch_gram.1 = (f32[640,640]{1,0:T(8,128)S(1)}, f32[16,16,8,128]{3,2,1,0:T(8,128)S(1)}) custom-call(s32[1]{0:T(128)S(6)} %copy.8.count, s32[1]{0:T(128)S(6)} %copy.7.index, f32[2048,256]{1,0:T(8,128)} %sketch_hbm.1, f32[256,512]{1,0:T(8,128)} %prior.1, f32[256,256]{1,0:T(8,128)} %panel.1), custom_call_target="tpu_custom_call" | custom-call | tf_op jit(solution)/shard_map/sketch_gram/pallas_call | solution.py:314
  70.0 0.0 copy-done.1
  70.0 0.0 copy-done
  70.0 21.5 %project.1 = (f32[256,128]{1,0:T(8,128)}, f32[640,128]{1,0:T(8,128)}) custom-call(s32[1]{0:T(128)S(6)} %copy.8.count, s32[1]{0:T(128)S(6)} %copy.7.index, f32[640,640]{1,0:T(8,128)S(1)} %get-tuple-element.4.gram, f32[16,16,8,128]{3,2,1,0:T(8,128)S(1)} %get-tuple-element.5.plain, f32[256,512]{1,0:T(8,128)S(1)} %copy-done, f32[256,256]{1,0:T(8,128)S(1)} %copy-done.1), custom_call_target="tpu_custom_call" | custom-call | tf_op jit(solution)/shard_map/project/pallas_call | solution.py:473
Async XLA Ops:
  0.6 69.3 %copy-start.1 = (f32[256,256]{1,0:T(8,128)S(1)}, f32[256,256]{1,0:T(8,128)}, u32[]{:S(2)}) copy-start(f32[256,256]{1,0:T(8,128)} %panel.1) | copy-start | bytes 786436
  0.6 69.3 %copy-start = (f32[256,512]{1,0:T(8,128)S(1)}, f32[256,512]{1,0:T(8,128)}, u32[]{:S(2)}) copy-start(f32[256,512]{1,0:T(8,128)} %prior.1) | copy-start | bytes 1572868

commit v5 on v4

--- a/solution.py
+++ b/solution.py
@@ -22,6 +22,27 @@
 
 def dot(left, right):
     return jnp.dot(left, right, precision=lax.Precision.HIGHEST, preferred_element_type=F32)
+
+
+def thirds(value):
+    high = value.astype(BF16)
+    rest = value - high.astype(F32)
+    middle = rest.astype(BF16)
+    return high, middle, (rest - middle.astype(F32)).astype(BF16)
+
+
+def deep(left, right, rows=False):
+    lh, lm, ll = thirds(left)
+    rh, rm, rl = thirds(right)
+    axis = 0 if rows else 1
+    dims = (((axis,), (0,)), ((), ()))
+    value = None
+    for pair, other in (((lh, ll), (rl, rh)), ((lh, lm), (rm, rh)), ((lh, lm), (rh, rm))):
+        term = lax.dot_general(
+            jnp.concatenate(pair, axis=axis), jnp.concatenate(other, axis=0), dims, preferred_element_type=F32
+        )
+        value = term if value is None else value + term
+    return value
 
 
 def dot_rows(left, right):
@@ -146,12 +167,12 @@
 
     for part in range(2):
         product(1 - c, parts[part], away)
-    product(c, parts[0], acc)
     pl.semaphore_wait(barrier, 16)
     for part in range(2):
         for s in range(8):
             chunk(part, s).start()
-    product(c, parts[1], acc)
+    for part in range(2):
+        product(c, parts[part], acc)
 
     landing = (r0, r1)
 
@@ -440,23 +461,23 @@
         hi = lo + 128
         unused = (c + lo >= count[0]) & (r == c)
         block = a[lo:hi, lo:hi] + jnp.where(unused, 1.0, 0.0)
-        y = dot(inverse_of(block), a[lo:hi, hi:])
+        y = deep(inverse_of(block), a[lo:hi, hi:])
         for i in range(k + 1, 5):
             left = 128 * i
-            a[left:left + 128, left:] -= dot_rows(a[lo:hi, left:left + 128], y[:, left - hi:])
+            a[left:left + 128, left:] -= deep(a[lo:hi, left:left + 128], y[:, left - hi:], True)
         if k:
-            a[:lo, hi:] -= dot(a[:lo, lo:hi], y)
+            a[:lo, hi:] -= deep(a[:lo, lo:hi], y)
         a[lo:hi, hi:] = y
     coefs = a[:512, 512:]
-    tail = a[512:, 512:]
-    both = eliminated(tail[:64], 0)
-    ratio = jnp.where(on_left, 0.0, both)
-    ends = (r == c).astype(F32) - jnp.concatenate([ratio, jnp.zeros((64, 128), F32)], axis=0)
-    weights = jnp.concatenate([dot(coefs[:, :P_SIZE], ratio) - coefs, ends], axis=0)
-    own = dot_rows(weights, dot(b[...], weights))
-    small = jnp.concatenate([own[:P_SIZE, :P_SIZE], own[P_SIZE:, P_SIZE:]], axis=1)
     keep = lax.broadcasted_iota(jnp.int32, (256, 512), 1) < count[0]
     resid = choose(panel, index[0]) - dot(jnp.where(keep, prior[...], 0.0), coefs)
+    weights = jnp.concatenate([-coefs, (r == c).astype(F32)], axis=0)
+    own = dot_rows(weights, dot(b[...], weights))
+    both = eliminated(a[512:576, 512:], 0)
+    ratio = jnp.where(on_left, 0.0, both)
+    own = own - dot(own[:, :P_SIZE], ratio)
+    own = own - dot_rows(ratio, own[:P_SIZE])
+    small = jnp.concatenate([own[:P_SIZE, :P_SIZE], own[P_SIZE:, P_SIZE:]], axis=1)
     resid = resid - dot(resid[:, :P_SIZE], ratio)
     tri, inverse = factor(small)
     both = jnp.concatenate([jnp.where(on_left, inverse, 0.0), jnp.where(on_left, 0.0, inverse)], axis=0)

time: 91.6 us -> 89.3 us (0.975)
  Pallas kernels: 89.5 us -> 87.2 us
    pallas_call x1, Pallas kernels: 21.5 us -> 20 us  [project(): pl.pallas_call(functools.partial(project_kernel, scale), out_shape=(jax.S...]
where the time goes in v5:
time: 89.3 us; the launch traced here: 89.2 us
  Pallas kernels  87.2 us (98%)
  between operations  2.03 us (2%)
    pallas_call x1, Pallas kernels, sketch_gram(): pl.pallas_call(gram_kernel, out_shape=(jax.ShapeDtypeStruct((640, 640), F...  67.2 us
    pallas_call x1, Pallas kernels, project(): pl.pallas_call(functools.partial(project_kernel, scale), out_shape=(jax.S...  20 us

profile of v5, /device:TPU:1, one launch (start us, length us, event | category | flops | bytes accessed | tf_op | source)
XLA Modules:
  0.0 89.2 jit_solution(13770688695656836517)
XLA Ops:
  0.6 0.0 copy-start.1
  0.6 0.0 copy-start
  2.0 67.2 %sketch_gram.1 = (f32[640,640]{1,0:T(8,128)S(1)}, f32[16,16,8,128]{3,2,1,0:T(8,128)S(1)}) custom-call(s32[1]{0:T(128)S(6)} %copy.8.count, s32[1]{0:T(128)S(6)} %copy.7.index, f32[2048,256]{1,0:T(8,128)} %sketch_hbm.1, f32[256,512]{1,0:T(8,128)} %prior.1, f32[256,256]{1,0:T(8,128)} %panel.1), custom_call_target="tpu_custom_call" | custom-call | tf_op jit(solution)/shard_map/sketch_gram/pallas_call | solution.py:335
  69.2 0.0 copy-done.1
  69.2 0.0 copy-done
  69.2 20.0 %project.1 = (f32[256,128]{1,0:T(8,128)}, f32[640,128]{1,0:T(8,128)}) custom-call(s32[1]{0:T(128)S(6)} %copy.8.count, s32[1]{0:T(128)S(6)} %copy.7.index, f32[640,640]{1,0:T(8,128)S(1)} %get-tuple-element.4.gram, f32[16,16,8,128]{3,2,1,0:T(8,128)S(1)} %get-tuple-element.5.plain, f32[256,512]{1,0:T(8,128)S(1)} %copy-done, f32[256,256]{1,0:T(8,128)S(1)} %copy-done.1), custom_call_target="tpu_custom_call" | custom-call | tf_op jit(solution)/shard_map/project/pallas_call | solution.py:494
Async XLA Ops:
  0.6 68.6 %copy-start.1 = (f32[256,256]{1,0:T(8,128)S(1)}, f32[256,256]{1,0:T(8,128)}, u32[]{:S(2)}) copy-start(f32[256,256]{1,0:T(8,128)} %panel.1) | copy-start | bytes 786436
  0.6 68.6 %copy-start = (f32[256,512]{1,0:T(8,128)S(1)}, f32[256,512]{1,0:T(8,128)}, u32[]{:S(2)}) copy-start(f32[256,512]{1,0:T(8,128)} %prior.1) | copy-start | bytes 1572868

commit v6 on v5

--- a/solution.py
+++ b/solution.py
@@ -400,9 +400,12 @@
 def inverse_of(block):
     on_left = lax.broadcasted_iota(jnp.int32, (64, 128), 1) < P_SIZE
     top = eliminated(block[:64], 0)
-    bottom = jnp.where(on_left, 0.0, block[64:]) - dot(block[64:, :64], top)
+    none = jnp.zeros((64, 128), F32)
+    bottom = jnp.where(on_left, 0.0, block[64:])
+    bottom = bottom - deep(block[64:] - bottom, jnp.concatenate([top, none], axis=0))
     bottom = eliminated(bottom, 64)
-    top = jnp.where(on_left, top, 0.0) - dot(top[:, 64:], bottom)
+    kept = jnp.where(on_left, top, 0.0)
+    top = kept - deep(top - kept, jnp.concatenate([none, bottom], axis=0))
     return jnp.concatenate([top, bottom], axis=0)
 
 

time: 89.3 us -> 89.2 us (level)
  no operation moved by 1% of the time
where the time goes in v6:
time: 89.2 us; the launch traced here: 89 us
  Pallas kernels  87 us (98%)
  between operations  2.03 us (2%)
    pallas_call x1, Pallas kernels, sketch_gram(): pl.pallas_call(gram_kernel, out_shape=(jax.ShapeDtypeStruct((640, 640), F...  67.2 us
    pallas_call x1, Pallas kernels, project(): pl.pallas_call(functools.partial(project_kernel, scale), out_shape=(jax.S...  19.8 us

profile of v6, /device:TPU:1, one launch (start us, length us, event | category | flops | bytes accessed | tf_op | source)
XLA Modules:
  0.0 89.0 jit_solution(11561434771577500458)
XLA Ops:
  0.6 0.0 copy-start.1
  0.6 0.0 copy-start
  2.0 67.2 %sketch_gram.1 = (f32[640,640]{1,0:T(8,128)S(1)}, f32[16,16,8,128]{3,2,1,0:T(8,128)S(1)}) custom-call(s32[1]{0:T(128)S(6)} %copy.8.count, s32[1]{0:T(128)S(6)} %copy.7.index, f32[2048,256]{1,0:T(8,128)} %sketch_hbm.1, f32[256,512]{1,0:T(8,128)} %prior.1, f32[256,256]{1,0:T(8,128)} %panel.1), custom_call_target="tpu_custom_call" | custom-call | tf_op jit(solution)/shard_map/sketch_gram/pallas_call | solution.py:335
  69.2 0.0 copy-done.1
  69.2 0.0 copy-done
  69.2 19.8 %project.1 = (f32[256,128]{1,0:T(8,128)}, f32[640,128]{1,0:T(8,128)}) custom-call(s32[1]{0:T(128)S(6)} %copy.8.count, s32[1]{0:T(128)S(6)} %copy.7.index, f32[640,640]{1,0:T(8,128)S(1)} %get-tuple-element.4.gram, f32[16,16,8,128]{3,2,1,0:T(8,128)S(1)} %get-tuple-element.5.plain, f32[256,512]{1,0:T(8,128)S(1)} %copy-done, f32[256,256]{1,0:T(8,128)S(1)} %copy-done.1), custom_call_target="tpu_custom_call" | custom-call | tf_op jit(solution)/shard_map/project/pallas_call | solution.py:497
Async XLA Ops:
  0.6 68.6 %copy-start.1 = (f32[256,256]{1,0:T(8,128)S(1)}, f32[256,256]{1,0:T(8,128)}, u32[]{:S(2)}) copy-start(f32[256,256]{1,0:T(8,128)} %panel.1) | copy-start | bytes 786436
  0.6 68.6 %copy-start = (f32[256,512]{1,0:T(8,128)S(1)}, f32[256,512]{1,0:T(8,128)}, u32[]{:S(2)}) copy-start(f32[256,512]{1,0:T(8,128)} %prior.1) | copy-start | bytes 1572868
